TPU v7x, 128 devices: a whole 4x4x4 slice. The times are simulated.
128 devices in a mesh: key: 4 (over x_hi, core), head: 16 (over z, y), batch: 2 (over x_lo).
Axes of the slice: x: 4 (x_hi: 2, x_lo: 2; x = x_hi * 2 + x_lo), y: 4, z: 4, core: 2. Of those that a mesh axis runs over, the one named last changes fastest.
Arguments:
- new_queries: bfloat16 [16, 16, 4, 1024], P('batch', 'head'), parts along dimension 0, may hold values from -6 to 6
- new_keys: bfloat16 [16, 16, 4, 1024], P('batch', 'head'), parts along dimension 0, may hold values from -0.8984375 to 0.8984375
- new_values: bfloat16 [16, 16, 4, 1024], P('batch', 'head'), parts along dimension 0, may hold values from -6 to 6
- decay_gate: float32 [16, 16, 4], P('batch', 'head'), parts along dimension 0, may hold values from 0.85 to 0.999
- write_gate: float32 [16, 16, 4], P('batch', 'head'), parts along dimension 0, may hold values from 0.2 to 1
- ridge_shift: float32 [16], P('head'), may hold values from 0.5 to 2
- norm_gain: float32 [16, 1024], P('head', 'key'), may hold values from 0.1 to 1.9
- cov_state: bfloat16 [16, 16, 1024, 1024], P('batch', 'head', 'key'), parts along dimension 0, may hold values from -1 to 42, as said below
- value_state: bfloat16 [16, 16, 1024, 1024], P('batch', 'head', None, 'key'), parts along dimension 0, may hold values from -0.1875 to 0.1875
- out_weight: bfloat16 [16, 1024, 8192], P('head', 'key'), may hold values from -0.0625 to 0.0625
Outputs:
- layer_out: bfloat16 [16, 4, 8192], P('batch', None, ('key', 'head')), parts along dimension 0
There are 2 independent parts, one for each index of `batch`. A program takes and returns all parts, laid end to end along the dimension named above; an argument that names none is the same for every part. Nothing has to cross between parts.
Inputs may be any that keep to these rules, and one draw needn't show every extreme that they name: `cov_state`: each 1024 x 1024 block is symmetric and positive definite.
All inputs are finite; a program needn't handle non-finite values.
Results may differ from a plain program's by a relative error of at most 0.0085.
Values may be sent and summed in bfloat16 or wider, within the bound.
No kernel may reach another device: no remote copies, remote signals or barrier semaphores. Data moves between devices by JAX's collectives and lax.ppermute only.
A program may use at most 64 MiB of HBM per device.

v0:
```python
import jax
import jax.numpy as jnp
from jax import lax
from jax.sharding import PartitionSpec as P

DRAFT = 4
ITERS = 3


def copy_for_each(x, axis):
    size = lax.axis_size(axis)
    return lax.all_to_all(jnp.broadcast_to(x[None], (size, *x.shape)), axis, 0, 0, tiled=True)


def of_everyone(x, axis):
    return copy_for_each(x, axis).sum(axis=0)


def split_up(x, dim, size):
    before, after = (x.shape[:dim], x.shape[dim + 1 :])
    return jnp.moveaxis(x.reshape(*before, size, -1, *after), dim, 0)


def sent_and_summed(x, axis, dim):
    pieces = split_up(x, dim, lax.axis_size(axis))
    arrived = lax.all_to_all(pieces, axis, split_axis=0, concat_axis=0, tiled=True)
    return arrived.astype(jnp.float32).sum(axis=0)


def coefficients(decay_gate, write_gate):
    decay_total = jnp.cumprod(decay_gate, axis=-1)
    decay_ratio = decay_total[..., :, None] / decay_total[..., None, :]
    is_later = jnp.arange(DRAFT)[:, None] >= jnp.arange(DRAFT)[None, :]
    mix_weights = jnp.where(
        is_later, write_gate[..., None, :] * decay_ratio, jnp.zeros_like(decay_ratio)
    )
    return (decay_total, mix_weights)


def body(
    new_queries,
    new_keys,
    new_values,
    decay_gate,
    write_gate,
    ridge_shift,
    norm_gain,
    cov_state,
    value_state,
    out_weight,
):
    high = lax.Precision.HIGHEST
    row_count = cov_state.shape[2]
    row_start = lax.axis_index("key") * row_count
    decay_total, mix_weights = coefficients(decay_gate, write_gate)
    ridge_term = ridge_shift[None, :, None, None]
    key_rows = lax.dynamic_slice_in_dim(new_keys, row_start, row_count, 3).astype(jnp.float32)
    residual = new_queries.astype(jnp.float32)
    direction = residual
    solution = jnp.zeros_like(residual)
    sq_norm = jnp.sum(residual * residual, axis=-1)
    for sweep_index in range(ITERS):
        dir_bf = direction.astype(jnp.bfloat16)
        dir_rows = lax.dynamic_slice_in_dim(direction, row_start, row_count, 3)
        state_prod = jnp.einsum(
            "shic,shtc->shti", cov_state, dir_bf, preferred_element_type=jnp.float32
        )
        key_dots = jnp.einsum(
            "shtc,shuc->shtu", dir_bf, new_keys, preferred_element_type=jnp.float32
        )
        low_rank = jnp.einsum("shtu,shuc->shtc", mix_weights * key_dots, key_rows, precision=high)
        applied = lax.all_gather(
            decay_total[..., None] * state_prod + low_rank + ridge_term * dir_rows,
            "key",
            axis=3,
            tiled=True,
        )
        step_size = sq_norm / jnp.sum(direction * applied, axis=-1)
        solution = solution + step_size[..., None] * direction
        residual = residual - step_size[..., None] * applied
        new_norm = jnp.sum(residual * residual, axis=-1)
        direction = residual + (new_norm / sq_norm)[..., None] * direction
        sq_norm = new_norm
    sol_rows = lax.dynamic_slice_in_dim(solution, row_start, row_count, 3)
    sol_bf = sol_rows.astype(jnp.bfloat16)
    state_read = jnp.einsum(
        "shvc,shtc->shtv", value_state, sol_bf, preferred_element_type=jnp.float32
    )
    key_sol = jnp.einsum("shtc,shuc->shtu", sol_bf.astype(jnp.float32), key_rows, precision=high)
    read_part = decay_total[..., None] * state_read + jnp.einsum(
        "shtu,shuv->shtv", mix_weights * key_sol, new_values.astype(jnp.float32), precision=high
    )
    value_count = value_state.shape[2]
    read_whole = of_everyone(read_part, "key")
    mean_sq = jnp.sum(read_whole * read_whole, axis=-1) / value_count
    val_rows = out_weight.shape[1]
    read_mine = lax.dynamic_slice_in_dim(read_whole, lax.axis_index("key") * val_rows, val_rows, 3)
    normed = (
        read_mine * lax.rsqrt(mean_sq + 1e-06)[..., None] * norm_gain[None, :, None, :]
    ).astype(jnp.bfloat16)
    partial_out = jnp.einsum(
        "shtv,hvm->stm", normed, out_weight, preferred_element_type=jnp.float32
    )
    summed = sent_and_summed(partial_out.astype(jnp.bfloat16), ("key", "head"), 2)
    return summed.astype(jnp.bfloat16)


def solution(mesh):
    placed = (
        P("batch", "head", None, None),
        P("batch", "head", None, None),
        P("batch", "head", None, None),
        P("batch", "head", None),
        P("batch", "head", None),
        P("head"),
        P("head", "key"),
        P("batch", "head", "key", None),
        P("batch", "head", None, "key"),
        P("head", "key", None),
    )
    return jax.shard_map(
        body,
        mesh=mesh,
        in_specs=placed,
        out_specs=P("batch", None, ("key", "head")),
        check_vma=False,
    )
```

profile of v0, /device:TPU:0, one launch (start us, length us, event | category | flops | bytes accessed | tf_op | source)
XLA Modules:
  0.0 77.1 jit_solution(10526807287161114871)
XLA Ops:
  0.0 0.0 copy-start
  0.0 0.0 copy-start.3
  0.0 0.0 copy-start.4
  0.7 0.7 reduce_window.12
  1.4 0.1 copy.26
  1.5 0.8 copy.29
  2.3 0.8 %bitcast_convert_fusion = f32[8,1,4,1024]{3,2,0,1:T(4,128)S(1)} fusion(bf16[8,1,4,1024]{3,2,1,0:T(4,128)(2,1)} %param.10), kind=kLoop, calls=%fused_computation.51 | loop fusion | flops 32768 | bytes 196608 | tf_op jit(solution)/shard_map/convert_element_type | solution.py:58
  3.1 0.0 copy-start.1
  3.1 1.2 %convolution_multiply_fusion.3 = f32[8,4,4]{2,1,0:T(4,128)S(1)} fusion(bf16[8,1,4,1024]{3,2,1,0:T(4,128)(2,1)} %param.11, bf16[8,1,4,1024]{3,2,1,0:T(4,128)(2,1)} %param.10, f32[8,4]{1,0:T(8,128)S(1)} %copy.26, f32[8,4]{1,0:T(8,128)S(1)} %copy.29, pred[4,4]{1,0:T(4,128)(4,1)S(1)} %iota_compare_fusion), kind=kOutput, calls=%fused_computation.28 | convolution fusion | flops 262656 | bytes 131856 | tf_op jit(solution)/shard_map/shtc,shuc->shtu/dot_general | solution.py:68
  4.3 1.0 %fusion.73 = f32[8,4,256]{2,1,0:T(4,128)S(1)} fusion(f32[8,4,4]{2,1,0:T(4,128)S(1)} %convolution_multiply_fusion.3, bf16[8,1,4,1024]{3,2,1,0:T(4,128)(2,1)} %param.11, s32[]{:T(128)S(6)} %select_n.14), kind=kOutput, calls=%fused_computation.67 | convolution fusion | flops 393216 | bytes 49668 | tf_op jit(solution)/shard_map/shtu,shuc->shtc/dot_general | solution.py:71
  5.3 3.4 %fusion.48 = f32[8,1,4,256]{3,2,0,1:T(4,128)S(1)} fusion(f32[8,4,256]{2,1,0:T(4,128)S(1)} %fusion.73, bf16[8,1,256,1024]{3,2,1,0:T(8,128)(2,1)} %param.17, bf16[8,1,4,1024]{3,2,1,0:T(4,128)(2,1)} %param.10, f32[8,1,4,1024]{3,2,0,1:T(4,128)S(1)} %bitcast_convert_fusion, s32[]{:T(128)S(6)} %select_n.14, f32[]{:T(128)} %bitcast.120, f32[8,4]{1,0:T(8,128)S(1)} %copy.26), kind=kOutput, calls=%fused_computation.24 | convolution fusion | flops 16809984 | bytes 4358280 | tf_op jit(solution)/shard_map/shic,shtc->shti/dot_general | solution.py:65
  8.7 6.9 %all_gather.9 = f32[8,1,4,1024]{3,2,0,1:T(4,128)S(1)} all-gather(f32[8,1,4,256]{3,2,0,1:T(4,128)S(1)} %fusion.48), channel_id=1, replica_groups=mesh['key'=4,'head'=16,'batch'=2] {'key'}, dimensions={3}, use_global_device_ids=true | all-gather | bytes 163840 | tf_op jit(solution)/shard_map/all_gather | solution.py:72
  15.7 0.0 copy-done.3
  15.7 0.1 multiply_reduce_fusion.5
  15.8 0.2 multiply_reduce_fusion.4
  16.0 0.1 multiply_add_fusion.1
  16.2 0.0 copy-done.4
  16.2 0.2 convolution_multiply_fusion.2
  16.4 0.2 fusion.71
  16.5 0.0 copy-done.1
  16.5 1.2 %fusion.45 = f32[8,1,4,256]{3,2,0,1:T(4,128)S(1)} fusion(f32[8,4,256]{2,1,0:T(4,128)S(1)} %fusion.71, bf16[8,1,256,1024]{3,2,1,0:T(8,128)(2,1)S(1)} %copy-done.1, f32[8,1,4,1024]{3,2,0,1:T(4,128)S(1)} %multiply_add_fusion.1, s32[]{:T(128)S(6)} %select_n.14, f32[]{:T(128)} %bitcast.122, f32[8,4]{1,0:T(8,128)S(1)} %copy.26), kind=kOutput, calls=%fused_computation.23 | convolution fusion | flops 16842752 | bytes 4427784 | tf_op jit(solution)/shard_map/shic,shtc->shti/dot_general | solution.py:65
  17.7 0.0 copy-start.2
  17.7 7.1 %all_gather.10 = f32[8,1,4,1024]{3,2,0,1:T(4,128)S(1)} all-gather(f32[8,1,4,256]{3,2,0,1:T(4,128)S(1)} %fusion.45), channel_id=1, replica_groups=mesh['key'=4,'head'=16,'batch'=2] {'key'}, dimensions={3}, use_global_device_ids=true | all-gather | bytes 163840 | tf_op jit(solution)/shard_map/all_gather | solution.py:72
  24.8 0.1 multiply_reduce_fusion.3
  24.9 0.2 multiply_reduce_fusion.2
  25.1 0.1 multiply_add_fusion
  25.3 0.2 convolution_multiply_fusion.1
  25.5 0.2 fusion.69
  25.6 1.2 %fusion.42 = f32[8,1,4,256]{3,2,0,1:T(4,128)S(1)} fusion(f32[8,4,256]{2,1,0:T(4,128)S(1)} %fusion.69, bf16[8,1,256,1024]{3,2,1,0:T(8,128)(2,1)S(1)} %copy-done.1, f32[8,1,4,1024]{3,2,0,1:T(4,128)S(1)} %multiply_add_fusion, s32[]{:T(128)S(6)} %select_n.14, f32[]{:T(128)} %bitcast.121, f32[8,4]{1,0:T(8,128)S(1)} %copy.26), kind=kOutput, calls=%fused_computation.22 | convolution fusion | flops 16842752 | bytes 4427784 | tf_op jit(solution)/shard_map/shic,shtc->shti/dot_general | solution.py:65
  26.8 0.0 copy-start.5
  26.8 7.1 %all_gather.11 = f32[8,1,4,1024]{3,2,0,1:T(4,128)S(1)} all-gather(f32[8,1,4,256]{3,2,0,1:T(4,128)S(1)} %fusion.42), channel_id=1, replica_groups=mesh['key'=4,'head'=16,'batch'=2] {'key'}, dimensions={3}, use_global_device_ids=true | all-gather | bytes 163840 | tf_op jit(solution)/shard_map/all_gather | solution.py:72
  33.9 0.1 multiply_reduce_fusion.1
  34.0 0.1 add_convert_fusion
  34.1 0.1 convolution_multiply_fusion
  34.2 0.0 copy-done.2
  34.3 1.2 %fusion.12 = f32[8,4,1024]{2,1,0:T(4,128)S(1)} fusion(bf16[8,1,1024,256]{3,2,1,0:T(8,128)(2,1)S(1)} %copy-done.2, f32[8,4]{1,0:T(8,128)S(1)} %copy.26, bf16[8,1,4,256]{3,2,0,1:T(4,128)(2,1)S(1)} %add_convert_fusion), kind=kOutput, calls=%fused_computation.12 | convolution fusion | flops 16809984 | bytes 4341888 | tf_op jit(solution)/shard_map/shvc,shtc->shtv/dot_general | solution.py:86
  35.4 0.0 copy-done
  35.4 0.3 convolution_add_fusion
  35.7 0.1 copy.32
  35.9 14.5 %all_to_all.10 = f32[4,8,1,4,1024]{4,1,3,2,0:T(8,128)S(1)} all-to-all(f32[4,8,1,4,1024]{4,1,3,2,0:T(8,128)S(1)} %broadcast_in_dim.10), channel_id=1, replica_groups=mesh['key'=4,'head'=16,'batch'=2] {'key'}, dimensions={0} | all-to-all | bytes 1048576 | tf_op jit(solution)/shard_map/all_to_all | solution.py:12
  50.4 0.1 multiply_reduce_fusion
  50.5 0.0 copy-done.5
  50.5 3.0 %fusion.9 = bf16[8,4,64,128]{3,0,2,1:T(8,128)(2,1)S(1)} fusion(bf16[1,256,8192]{2,1,0:T(8,128)(2,1)} %param.19, f32[8,4,1024]{2,0,1:T(8,128)S(1)} %reduce_sum.90, s32[]{:T(128)S(6)} %select_n.14, f32[256]{0:T(256)S(1)} %bitcast.124, f32[8,4]{0,1:T(4,128)S(1)} %add_rsqrt_fusion), kind=kOutput, calls=%fused_computation.10 | convolution fusion | flops 134504448 | bytes 4754436 | tf_op jit(solution)/shard_map/shtv,hvm->stm/dot_general | solution.py:101
  53.6 0.1 copy.38
  53.7 22.7 %all_to_all.11 = bf16[64,8,4,128]{3,1,2,0:T(8,128)(2,1)S(1)} all-to-all(bf16[64,8,4,128]{3,1,2,0:T(8,128)(2,1)S(1)} %bitcast.123), channel_id=1, replica_groups=mesh['key'=4,'head'=16,'batch'=2] {'key','head'}, dimensions={0} | all-to-all | bytes 1048576 | tf_op jit(solution)/shard_map/all_to_all | solution.py:26
  76.4 0.1 reduce_sum.92
  76.5 0.6 copy.35
  (9 shorter events, 0.1 us)
Async XLA Ops:
  0.0 35.4 %copy-start = (bf16[8,1,4,1024]{3,2,1,0:T(4,128)(2,1)S(1)}, bf16[8,1,4,1024]{3,2,1,0:T(4,128)(2,1)}, u32[]{:S(2)}) copy-start(bf16[8,1,4,1024]{3,2,1,0:T(4,128)(2,1)} %param.12) | copy-start | bytes 196612
  0.0 15.7 %copy-start.3 = (bf16[8,1,4,1024]{3,2,1,0:T(4,128)(2,1)S(1)}, bf16[8,1,4,1024]{3,2,1,0:T(4,128)(2,1)}, u32[]{:S(2)}) copy-start(bf16[8,1,4,1024]{3,2,1,0:T(4,128)(2,1)} %param.10) | copy-start | bytes 196612
  0.0 16.2 %copy-start.4 = (bf16[8,1,4,1024]{3,2,1,0:T(4,128)(2,1)S(1)}, bf16[8,1,4,1024]{3,2,1,0:T(4,128)(2,1)}, u32[]{:S(2)}) copy-start(bf16[8,1,4,1024]{3,2,1,0:T(4,128)(2,1)} %param.11) | copy-start | bytes 196612
  3.1 13.4 %copy-start.1 = (bf16[8,1,256,1024]{3,2,1,0:T(8,128)(2,1)S(1)}, bf16[8,1,256,1024]{3,2,1,0:T(8,128)(2,1)}, u32[]{:S(2)}) copy-start(bf16[8,1,256,1024]{3,2,1,0:T(8,128)(2,1)} %param.17) | copy-start | bytes 12582916
  17.7 16.5 %copy-start.2 = (bf16[8,1,1024,256]{3,2,1,0:T(8,128)(2,1)S(1)}, bf16[8,1,1024,256]{3,2,1,0:T(8,128)(2,1)}, u32[]{:S(2)}) copy-start(bf16[8,1,1024,256]{3,2,1,0:T(8,128)(2,1)} %param.18) | copy-start | bytes 12582916
  26.8 23.7 %copy-start.5 = (f32[1,256]{1,0:T(1,128)S(1)}, f32[1,256]{1,0:T(1,128)}, u32[]{:S(2)}) copy-start(f32[1,256]{1,0:T(1,128)} %param.16) | copy-start | bytes 3076
where the time goes:
time: 77.5 us; the launch traced here: 77.1 us
  blocking collectives  58.3 us (75%)
  matrix products  13.3 us (17%)
  other arithmetic  3 us (4%)
  local copies, waits for them, and re-layouts  1.7 us (2%)
  between operations  0.82 us (1%)
    all_to_all x1, blocking collectives, sent_and_summed(): lax.all_to_all(pieces, axis, split_axis=0, concat_axis=0, tiled=True)  22.7 us
    all_gather x3, blocking collectives, body(): lax.all_gather(decay_total[..., None] * state_prod + low_rank + ridge_ter...  21 us
    all_to_all x1, blocking collectives, copy_for_each(): lax.all_to_all(jnp.broadcast_to(x[None], (size, *x.shape)), axis, 0, 0, t...  14.5 us
    dot_general x3, matrix products, body(): jnp.einsum('shic,shtc->shti', cov_state, dir_bf, preferred_element_type=j...  5.8 us
    dot_general x1, matrix products, body(): jnp.einsum('shtv,hvm->stm', normed, out_weight, preferred_element_type=jn...  3.03 us
    dot_general x3, matrix products, body(): jnp.einsum('shtc,shuc->shtu', dir_bf, new_keys, preferred_element_type=jn...  1.58 us

commit v1 on v0

v1 whole, which is shorter than its diff:
```python
import functools

import jax
import jax.numpy as jnp
from jax import lax
from jax.experimental import pallas as pl
from jax.experimental.pallas import tpu as pltpu
from jax.sharding import Mesh, PartitionSpec as P

DRAFT = 4
SEQS = 8
ROWS = SEQS * DRAFT
DK = 1024
DV = 1024
PART = 256
HEADS = 16
F32 = jnp.float32
BF16 = jnp.bfloat16
KEY = ("xh", "core")
HBM = pl.BlockSpec(memory_space=pltpu.HBM)
VMEM = pl.BlockSpec(memory_space=pltpu.VMEM)
SMEM = pl.BlockSpec(memory_space=pltpu.SMEM)
NT = (((1,), (1,)), ((), ()))
NN = (((1,), (0,)), ((), ()))


def mm(a, b, dims=NN):
    return lax.dot_general(a, b, dims, preferred_element_type=F32)


def halves(x):
    hi = x.astype(BF16)
    return hi, (x - hi.astype(F32)).astype(BF16)


def mm_wide(a, b):
    hi, lo = halves(a)
    return mm(hi, b) + mm(lo, b)


def coefficients(decay, write):
    totals = [decay[0:1]]
    for t in range(1, DRAFT):
        totals.append(totals[-1] * decay[t : t + 1])
    row = lax.broadcasted_iota(jnp.int32, (ROWS, SEQS), 0)
    seq = lax.broadcasted_iota(jnp.int32, (ROWS, SEQS), 1)
    token = row % DRAFT

    def column(rows):
        spread = jnp.zeros((ROWS, SEQS), F32)
        for t in range(DRAFT):
            spread = jnp.where(token == t, jnp.broadcast_to(rows[t], (ROWS, SEQS)), spread)
        return jnp.sum(jnp.where(row // DRAFT == seq, spread, 0.0), axis=1, keepdims=True)

    total = column(totals)
    written = column([write[t : t + 1] for t in range(DRAFT)])
    i = lax.broadcasted_iota(jnp.int32, (ROWS, ROWS), 0)
    j = lax.broadcasted_iota(jnp.int32, (ROWS, ROWS), 1)

    def as_row(col):
        return jnp.sum(jnp.where(i == j, jnp.broadcast_to(col, (ROWS, ROWS)), 0.0), axis=0, keepdims=True)

    kept = (i // DRAFT == j // DRAFT) & (j <= i)
    mix = jnp.where(kept, as_row(written) * (total / as_row(total)), 0.0)
    return total, mix


def stack(ref, out):
    for s in range(SEQS):
        out[DRAFT * s : DRAFT * (s + 1), :] = ref[s].astype(F32)


def first_kernel(
    me, ridge, q_hbm, k_hbm, decay_hbm, write_hbm, cov_hbm, msg,
    q_in, k_in, decay_in, write_in, cov, q32, k32, z32, small_sem, cov_sem,
):
    small = [
        pltpu.make_async_copy(a, b, small_sem.at[n])
        for n, (a, b) in enumerate(
            [(q_hbm, q_in), (k_hbm, k_in), (decay_hbm, decay_in), (write_hbm, write_in)]
        )
    ]
    big = [pltpu.make_async_copy(cov_hbm.at[s], cov.at[s], cov_sem.at[s]) for s in range(SEQS)]
    for c in small + big:
        c.start()
    for c in small:
        c.wait()
    total, mix = coefficients(decay_in[...], write_in[...])
    stack(q_in, q32)
    stack(k_in, k32)
    start = pl.multiple_of(me[0] * PART, PART)
    keys = k32[...].astype(BF16)
    keys_mine = k32[:, pl.ds(start, PART)].astype(BF16)
    dots = mm(q32[...].astype(BF16), keys, NT)
    base = mm_wide(mix * dots, keys_mine) + ridge[0] * q32[:, pl.ds(start, PART)]
    first = lax.broadcasted_iota(jnp.int32, (8, 1), 0) < DRAFT

    def by_columns(p, pieces):
        both = jnp.concatenate(pieces, axis=0)
        res = [mm(both, cov[2 * p + n]) for n in range(2)]
        z = jnp.where(first, res[0][:8] + res[0][8:], res[1][:8] + res[1][8:])
        z32[8 * p : 8 * p + 8, :] = z * total[8 * p : 8 * p + 8]

    held = None
    for p in range(SEQS // 2):
        big[2 * p].wait()
        big[2 * p + 1].wait()
        slab = q32[8 * p : 8 * p + 8, :].astype(BF16)
        res = [mm(slab, cov[2 * p + n], NT) for n in range(2)]
        y = jnp.where(first, res[0], res[1]) * total[8 * p : 8 * p + 8] + base[8 * p : 8 * p + 8]
        pieces = halves(y)
        msg[8 * p : 8 * p + 8, DK : DK + PART] = pieces[0]
        msg[8 * p : 8 * p + 8, DK + PART :] = pieces[1]
        if held is not None:
            by_columns(*held)
        held = (p, pieces)
    by_columns(*held)
    y_hi, y_lo = msg[:, DK : DK + PART], msg[:, DK + PART :]
    dots = mm(y_hi, keys_mine, NT) + mm(y_lo, keys_mine, NT)
    msg[:, :DK] = (z32[...] + mm_wide(mix * dots, keys)).astype(BF16)


def second_kernel(
    me, ridge, gathered, q_in, k_in, v_in, decay_in, write_in, cov, val, sent, kept,
    q32, k32, v32, d32, x32, r1, r2, quad32,
):
    total, mix = coefficients(decay_in[...], write_in[...])
    stack(q_in, q32)
    stack(k_in, k32)
    stack(v_in, v32)
    start = pl.multiple_of(me[0] * PART, PART)
    core, xh = me[1], me[2]

    def dot(a, b):
        return jnp.sum(a * b, axis=1, keepdims=True)

    q = q32[...]
    y = jnp.concatenate(
        [
            gathered[g, :, DK : DK + PART].astype(F32) + gathered[g, :, DK + PART :].astype(F32)
            for g in range(4)
        ],
        axis=1,
    )
    w = ridge[0] * y
    for g in range(4):
        w = w + gathered[g, :, :DK].astype(F32)
    rr0 = dot(q, q)
    a0 = rr0 / dot(q, y)
    res1 = q - a0 * y
    rr1 = dot(res1, res1)
    b0 = rr1 / rr0
    dir1 = res1 + b0 * q
    image = (1.0 + b0) * y - a0 * w
    a1 = rr1 / dot(dir1, image)
    sol2 = a0 * q + a1 * dir1
    res2 = res1 - a1 * image
    rr2 = dot(res2, res2)
    dir2 = res2 + (rr2 / rr1) * dir1
    d32[...] = dir2
    x32[...] = sol2
    keys = k32[...].astype(BF16)
    d_bf, x_bf = dir2.astype(BF16), sol2.astype(BF16)
    dots_d = mm(d_bf, keys, NT)
    dots_x = mm(x_bf, keys, NT)
    local = jnp.sum(mix * dots_d * dots_d, axis=1, keepdims=True) + ridge[0] * dot(dir2, dir2)
    first = lax.broadcasted_iota(jnp.int32, (8, 1), 0) < DRAFT
    for p in range(SEQS // 2):
        rows = slice(8 * p, 8 * p + 8)
        lhs = jnp.concatenate(halves(d32[rows, :]), axis=0)
        res = [mm(lhs, cov[2 * p + n], NT) for n in range(2)]
        t = jnp.where(first, res[0][:8] + res[0][8:], res[1][:8] + res[1][8:])
        quad32[rows, :] = t * d32[rows, pl.ds(start, PART)]
    for p in range(SEQS // 2):
        rows = slice(8 * p, 8 * p + 8)
        lhs = jnp.concatenate(
            [x32[rows, pl.ds(start, PART)].astype(BF16), d32[rows, pl.ds(start, PART)].astype(BF16)], axis=0
        )
        res = [mm(lhs, val[2 * p + n], NT) for n in range(2)]
        r1[rows, :] = jnp.where(first, res[0][:8], res[1][:8]) * total[rows]
        r2[rows, :] = jnp.where(first, res[0][8:], res[1][8:]) * total[rows]
    values = v32[:, pl.ds(start, PART)].astype(BF16)
    r1[:, pl.ds(start, PART)] += mm_wide(mix * dots_x, values)
    r2[:, pl.ds(start, PART)] += mm_wide(mix * dots_d, values)
    share = (total * jnp.sum(quad32[...], axis=1, keepdims=True) + 0.25 * local) / rr2
    share = jnp.broadcast_to(share, (ROWS, 128))
    for out, c in ((sent, 1 - core), (kept, core)):
        for x in range(2):
            cols = pl.ds(pl.multiple_of((2 * x + c) * PART, PART), PART)
            out[:, x * PART : (x + 1) * PART] = r1[:, cols].astype(out.dtype)
            out[:, (2 + x) * PART : (3 + x) * PART] = r2[:, cols].astype(out.dtype)
        out[:, 4 * PART :] = share.astype(out.dtype)


def third_kernel(me, mine, arrived, gain, weight, sent, kept):
    core, xh = me[1], me[2]
    total = mine[...].astype(F32) + arrived[...].astype(F32)
    a2 = 1.0 / total[:, 4 * PART : 4 * PART + 1]
    readout = total[:, : 2 * PART] + a2 * total[:, 2 * PART : 4 * PART]
    squares = jnp.broadcast_to(jnp.sum(readout * readout, axis=1, keepdims=True), (ROWS, 128))
    own = jnp.where(xh == 0, readout[:, :PART], readout[:, PART:])
    scaled = (own * gain[...]).astype(BF16)
    step = 512
    for out, c in ((sent, 1 - core), (kept, core)):
        for x in range(2):
            for n in range(2048 // step):
                cols = pl.ds(pl.multiple_of((2 * x + c) * 2048 + n * step, step), step)
                part = mm(scaled, weight[:, cols])
                for m in range(step // 128):
                    out[16 * x + n * (step // 128) + m] = part[:, 128 * m : 128 * (m + 1)].astype(out.dtype)
        hi, lo = halves(squares)
        out[32] = hi.astype(out.dtype)
        out[33] = lo.astype(out.dtype)


def swapped(x, axis):
    return lax.ppermute(x, axis, [(0, 1), (1, 0)])


def params(mib):
    return pltpu.CompilerParams(vmem_limit_bytes=mib << 20)


def body(
    new_queries, new_keys, new_values, decay_gate, write_gate,
    ridge_shift, norm_gain, cov_state, value_state, out_weight,
):
    xh, core = lax.axis_index("xh"), lax.axis_index("core")
    me = jnp.stack([2 * xh + core, core, xh]).astype(jnp.int32)
    q, k, v = (x[:, 0] for x in (new_queries, new_keys, new_values))
    decay, write = (x[:, 0].T for x in (decay_gate, write_gate))
    cov, val, weight = cov_state[:, 0], value_state[:, 0], out_weight[0]

    msg = pl.pallas_call(
        first_kernel,
        name="first",
        out_shape=jax.ShapeDtypeStruct((ROWS, DK + 2 * PART), BF16),
        in_specs=[SMEM, SMEM] + [HBM] * 5,
        out_specs=VMEM,
        scratch_shapes=[
            pltpu.VMEM((SEQS, DRAFT, DK), BF16),
            pltpu.VMEM((SEQS, DRAFT, DK), BF16),
            pltpu.VMEM((DRAFT, SEQS), F32),
            pltpu.VMEM((DRAFT, SEQS), F32),
            pltpu.VMEM((SEQS, PART, DK), BF16),
            pltpu.VMEM((ROWS, DK), F32),
            pltpu.VMEM((ROWS, DK), F32),
            pltpu.VMEM((ROWS, DK), F32),
            pltpu.SemaphoreType.DMA((4,)),
            pltpu.SemaphoreType.DMA((SEQS,)),
        ],
        compiler_params=params(16),
    )(me, ridge_shift, q, k, decay, write, cov)
    gathered = lax.all_gather(msg, KEY)
    sent, kept = pl.pallas_call(
        second_kernel,
        name="second",
        out_shape=(
            jax.ShapeDtypeStruct((ROWS, 4 * PART + 128), BF16),
            jax.ShapeDtypeStruct((ROWS, 4 * PART + 128), F32),
        ),
        in_specs=[SMEM, SMEM] + [VMEM] * 8,
        out_specs=(VMEM, VMEM),
        scratch_shapes=[pltpu.VMEM((ROWS, DK), F32) for _ in range(7)] + [pltpu.VMEM((ROWS, PART), F32)],
        compiler_params=params(24),
    )(me, ridge_shift, gathered, q, k, v, decay, write, cov, val)
    pair = (kept + swapped(sent, "core").astype(F32)).astype(BF16)
    other = swapped(pair, "xh")
    sent, kept = pl.pallas_call(
        third_kernel,
        name="third",
        out_shape=(
            jax.ShapeDtypeStruct((34, ROWS, 128), BF16),
            jax.ShapeDtypeStruct((34, ROWS, 128), F32),
        ),
        in_specs=[SMEM] + [VMEM] * 4,
        out_specs=(VMEM, VMEM),
        compiler_params=params(24),
    )(me, pair, other, norm_gain, weight)
    arrived = swapped(sent, "core").astype(F32)
    squares = kept[32] + kept[33] + arrived[32] + arrived[33]
    scale = lax.rsqrt(squares * (1.0 / DV) + 1e-06)
    part = ((kept[:32] + arrived[:32]) * scale).astype(BF16)
    landed = lax.all_to_all(part, ("xh", "head"), 0, 0, tiled=True)
    out = landed.astype(F32).sum(axis=0).astype(BF16)
    return out.reshape(SEQS, DRAFT, 128)


def solution(mesh):
    fine = Mesh(mesh.devices.reshape(2, 2, *mesh.devices.shape[1:]), ("xh", "core", "head", "batch"))
    placed = (
        P("batch", "head", None, None),
        P("batch", "head", None, None),
        P("batch", "head", None, None),
        P("batch", "head", None),
        P("batch", "head", None),
        P("head"),
        P("head", KEY),
        P("batch", "head", KEY, None),
        P("batch", "head", None, KEY),
        P("head", KEY, None),
    )
    return jax.shard_map(
        body,
        mesh=fine,
        in_specs=placed,
        out_specs=P("batch", None, ("xh", "core", "head")),
        check_vma=False,
    )
```

time: 77.5 us -> 56.2 us (0.73)
  blocking collectives: 58.3 us -> 29.2 us
  matrix products: 13.3 us -> 0 us
  Pallas kernels: 0 us -> 8.46 us
  waiting for transfers between devices: 0 us -> 5.81 us
  local copies, waits for them, and re-layouts: 1.7 us -> 7.44 us
  starting transfers between devices: 0 us -> 3.25 us
  other arithmetic: 3 us -> 0.91 us
    all_to_all x2 -> x1, blocking collectives: 37.3 us -> 21.1 us  [body(): landed = lax.all_to_all(part, ('xh', 'head'), 0, 0, tiled=True)]
    dot_general x13 -> x0, matrix products: 13.3 us -> none  [the longest x3 5.8 us: body(): jnp.einsum('shic,shtc->shti', cov_state, dir_bf, preferred_element_type=j...]
    all_gather x3 -> x1, blocking collectives: 21 us -> 8.1 us  [body(): gathered = lax.all_gather(msg, KEY)]
    pallas_call x0 -> x3, Pallas kernels: none -> 8.46 us  [the longest x1 3.73 us: body(): pl.pallas_call(first_kernel, name='first', out_shape=jax.ShapeDtypeStruct...]
    unnamed x12 -> x28, local copies, waits for them, and re-layouts: 0.03 us -> 7.44 us
    ppermute x0 -> x3, waiting for transfers between devices: none -> 5.81 us  [swapped(): return lax.ppermute(x, axis, [(0, 1), (1, 0)])]
    ppermute x0 -> x3, starting transfers between devices: none -> 3.25 us  [swapped(): return lax.ppermute(x, axis, [(0, 1), (1, 0)])]
  transfers between devices with their start and end apart: 0 -> 3, of which waited for: 0 -> 3; matrix products, arithmetic and copies ran while one was open for 0% -> 0% of each run, Pallas kernels for 0% -> 0%
where the time goes in v1:
time: 56.2 us; the launch traced here: 55.8 us
  blocking collectives  29.2 us (52%)
  Pallas kernels  8.46 us (15%)
  local copies, waits for them, and re-layouts  7.44 us (13%)
  waiting for transfers between devices  5.81 us (10%)
  starting transfers between devices  3.25 us (6%)
  other arithmetic  0.91 us (2%)
  between operations  0.78 us (1%)
    all_to_all x1, blocking collectives, body(): landed = lax.all_to_all(part, ('xh', 'head'), 0, 0, tiled=True)  21.1 us
    all_gather x1, blocking collectives, body(): gathered = lax.all_gather(msg, KEY)  8.1 us
    unnamed x28, local copies, waits for them, and re-layouts  7.44 us
    ppermute x3, waiting for transfers between devices, swapped(): return lax.ppermute(x, axis, [(0, 1), (1, 0)])  5.81 us
    pallas_call x1, Pallas kernels, body(): pl.pallas_call(first_kernel, name='first', out_shape=jax.ShapeDtypeStruct...  3.73 us
    pallas_call x1, Pallas kernels, body(): pl.pallas_call(second_kernel, name='second', out_shape=(jax.ShapeDtypeStr...  3.31 us
    ppermute x3, starting transfers between devices, swapped(): return lax.ppermute(x, axis, [(0, 1), (1, 0)])  3.25 us
    pallas_call x1, Pallas kernels, body(): pl.pallas_call(third_kernel, name='third', out_shape=(jax.ShapeDtypeStruc...  1.42 us
  transfers between devices with their start and end apart: 3, of which 3 were waited for; matrix products, arithmetic and copies ran while one was open for 0% of the time, Pallas kernels for 0%

profile of v1, /device:TPU:0, one launch (start us, length us, event | category | flops | bytes accessed | tf_op | source)
XLA Modules:
  0.0 55.8 jit_solution(5828964047061781335)
XLA Ops:
  0.0 0.0 copy-start.12
  0.0 0.0 copy-start.10
  0.7 0.1 pad_add_fusion.me
  0.8 0.0 copy-start
  0.8 2.2 %copy-done = bf16[8,1,256,1024]{3,2,1,0:T(8,128)(2,1)S(1)} copy-done((bf16[8,1,256,1024]{3,2,1,0:T(8,128)(2,1)S(1)}, bf16[8,1,256,1024]{3,2,1,0:T(8,128)(2,1)}, u32[]{:S(2)}) %copy-start) | copy-done | bytes 4194328
  3.0 0.0 copy-start.4
  3.0 0.8 %copy-done.4 = bf16[8,1,4,1024]{3,2,1,0:T(4,128)(2,1)S(1)} copy-done((bf16[8,1,4,1024]{3,2,1,0:T(4,128)(2,1)S(1)}, bf16[8,1,4,1024]{3,2,1,0:T(4,128)(2,1)}, u32[]{:S(2)}) %copy-start.4) | copy-done | bytes 65560
  3.8 0.0 copy-start.6
  3.8 0.8 %copy-done.6 = bf16[8,1,4,1024]{3,2,1,0:T(4,128)(2,1)S(1)} copy-done((bf16[8,1,4,1024]{3,2,1,0:T(4,128)(2,1)S(1)}, bf16[8,1,4,1024]{3,2,1,0:T(4,128)(2,1)}, u32[]{:S(2)}) %copy-start.6) | copy-done | bytes 65560
  4.6 0.0 copy-start.9
  4.6 0.7 %copy-done.9 = f32[8,1,4]{0,2,1:T(4,128)S(1)} copy-done((f32[8,1,4]{0,2,1:T(4,128)S(1)}, f32[8,1,4]{0,2,1:T(4,128)}, u32[]{:S(2)}) %copy-start.9) | copy-done | bytes 152
  5.3 0.0 copy-start.11
  5.3 0.7 %copy-done.11 = f32[8,1,4]{0,2,1:T(4,128)S(1)} copy-done((f32[8,1,4]{0,2,1:T(4,128)S(1)}, f32[8,1,4]{0,2,1:T(4,128)}, u32[]{:S(2)}) %copy-start.11) | copy-done | bytes 152
  6.0 0.0 copy-start.1
  6.0 0.0 copy-start.5
  6.0 0.0 copy-start.7
  6.0 0.0 copy-start.8
  6.0 3.7 %first.1 = bf16[32,1536]{1,0:T(8,128)(2,1)S(1)} custom-call(s32[3]{0:T(128)S(1)} %pad_add_fusion.me, f32[1]{0:T(128)S(6)} %copy.11.ridge, bf16[8,4,1024]{2,1,0:T(4,128)(2,1)S(1)} %bitcast.24, bf16[8,4,1024]{2,1,0:T(4,128)(2,1)S(1)} %bitcast.26, f32[4,8]{1,0:T(4,128)S(1)} %bitcast.29, f32[4,8]{1,0:T(4,128)S(1)} %bitcast.31, bf16[8,256,1024]{2,1,0:T(8,128)(2,1)S(1)} %bitcast.19), custom_call_target="tpu_custom_call" | custom-call | tf_op jit(solution)/shard_map/first/pallas_call | solution.py:234
  9.7 8.1 %all-gather = bf16[128,1536]{1,0:T(8,128)(2,1)S(1)} all-gather(bf16[32,1536]{1,0:T(8,128)(2,1)S(1)} %first.1), channel_id=2, replica_groups=mesh['xh'=2,'core'=2,'head'=16,'batch'=2] {'xh','core'}, dimensions={0}, use_global_device_ids=true | all-gather | bytes 491520 | tf_op jit(solution)/shard_map/all_gather | solution.py:254
  17.8 0.0 copy-done.12
  17.8 0.0 copy-done.10
  17.9 0.0 copy-done.1
  17.9 0.0 copy-done.5
  17.9 0.0 copy-done.7
  17.9 0.0 copy-done.8
  17.9 0.0 copy-start.3
  17.9 2.2 %copy-done.3 = bf16[8,1,1024,256]{3,2,1,0:T(8,128)(2,1)S(1)} copy-done((bf16[8,1,1024,256]{3,2,1,0:T(8,128)(2,1)S(1)}, bf16[8,1,1024,256]{3,2,1,0:T(8,128)(2,1)}, u32[]{:S(2)}) %copy-start.3) | copy-done | bytes 4194328
  20.1 0.0 copy-start.2
  20.1 0.0 copy-start.13
  20.1 3.3 %second.1 = (bf16[32,1152]{1,0:T(8,128)(2,1)S(1)}, f32[32,1152]{1,0:T(8,128)S(1)}) custom-call(s32[3]{0:T(128)S(1)} %pad_add_fusion.me, f32[1]{0:T(128)S(6)} %copy.11.ridge, bf16[4,32,1536]{2,1,0:T(8,128)(2,1)S(1)} %bitcast.23, bf16[8,4,1024]{2,1,0:T(4,128)(2,1)S(1)} %bitcast.25, bf16[8,4,1024]{2,1,0:T(4,128)(2,1)S(1)} %bitcast.27, ...), custom_call_target="tpu_custom_call" | custom-call | tf_op jit(solution)/shard_map/second/pallas_call | solution.py:255
  23.4 0.4 collective-permute-start
  23.8 0.9 %collective-permute-done = bf16[32,1152]{1,0:T(8,128)(2,1)S(1)} collective-permute-done((bf16[32,1152]{1,0:T(8,128)(2,1)S(1)}, bf16[32,1152]{1,0:T(8,128)(2,1)S(1)}, u32[]{:S(2)}, u32[]{:S(2)}) %collective-permute-start) | collective-permute-done | bytes 73760 | tf_op jit(solution)/shard_map/ppermute | solution.py:217
  24.8 2.8 %collective-permute-start.1 = (bf16[32,1152]{1,0:T(8,128)(2,1)S(1)}, bf16[32,1152]{1,0:T(8,128)(2,1)S(1)}, u32[]{:S(2)}, u32[]{:S(2)}) collective-permute-start(bf16[32,1152]{1,0:T(8,128)(2,1)S(1)} %add_convert_fusion.mine), channel_id=1, source_target_pairs={{0,64},{64,0},{1,65},{65,1},{2,66},{66,2},{3,67},{67,3},{4,68},{68... | collective-permute-start | bytes 221192 | tf_op jit(solution)/shard_map/ppermute | solution.py:217
  27.5 3.4 %collective-permute-done.1.arrived = bf16[32,1152]{1,0:T(8,128)(2,1)S(1)} collective-permute-done((bf16[32,1152]{1,0:T(8,128)(2,1)S(1)}, bf16[32,1152]{1,0:T(8,128)(2,1)S(1)}, u32[]{:S(2)}, u32[]{:S(2)}) %collective-permute-start.1) | collective-permute-done | bytes 73760 | tf_op jit(solution)/shard_map/ppermute | solution.py:217
  30.9 0.0 copy-done.2
  30.9 0.0 copy-done.13
  30.9 1.4 %third.1 = (bf16[34,32,128]{2,1,0:T(8,128)(2,1)S(1)}, f32[34,32,128]{2,1,0:T(8,128)S(1)}) custom-call(s32[3]{0:T(128)S(1)} %pad_add_fusion.me, bf16[32,1152]{1,0:T(8,128)(2,1)S(1)} %add_convert_fusion.mine, bf16[32,1152]{1,0:T(8,128)(2,1)S(1)} %collective-permute-done.1.arrived, f32[1,256]{1,0:T(1,128)S(1)} %copy-done.13, bf16[256,8192]{1,0:T(8,128)(2,1)S(1)} %bitcast.21), custom_call_target="tpu_custom_call" | custom-call | tf_op jit(solution)/shard_map/third/pallas_call | solution.py:269
  32.3 0.1 collective-permute-start.2
  32.4 1.5 %collective-permute-done.2 = bf16[34,32,128]{2,1,0:T(8,128)(2,1)S(1)} collective-permute-done((bf16[34,32,128]{2,1,0:T(8,128)(2,1)S(1)}, bf16[34,32,128]{2,1,0:T(8,128)(2,1)S(1)}, u32[]{:S(2)}, u32[]{:S(2)}) %collective-permute-start.2) | collective-permute-done | bytes 278560 | tf_op jit(solution)/shard_map/ppermute | solution.py:217
  33.9 0.1 convert_element_type.16
  34.0 0.1 fusion.1
  34.1 21.1 %all_to_all.5 = bf16[32,32,128]{2,1,0:T(8,128)(2,1)S(1)} all-to-all(bf16[32,32,128]{2,1,0:T(8,128)(2,1)S(1)} %fusion.1), channel_id=1, replica_groups=mesh['xh'=2,'core'=2,'head'=16,'batch'=2] {'xh','head'}, dimensions={0} | all-to-all | bytes 524288 | tf_op jit(solution)/shard_map/all_to_all | solution.py:284
  55.2 0.6 %reduce_sum.12 = bf16[32,128]{1,0:T(8,128)(2,1)} reduce(bf16[32,32,128]{2,1,0:T(8,128)(2,1)S(1)} %all_to_all.5, bf16[]{:T(256)} %constant.18.clone.1), dimensions={0}, to_apply=%region_0.0 | reduce | flops 126976 | bytes 270338 | tf_op jit(solution)/shard_map/reduce_sum | solution.py:285
  (2 shorter events, 0.0 us)
Async XLA Ops:
  0.0 17.8 %copy-start.12 = (f32[8,1,4]{0,2,1:T(4,128)S(1)}, f32[8,1,4]{0,2,1:T(4,128)}, u32[]{:S(2)}) copy-start(f32[8,1,4]{0,2,1:T(4,128)} %param.14) | copy-start | bytes 388
  0.0 17.8 %copy-start.10 = (f32[8,1,4]{0,2,1:T(4,128)S(1)}, f32[8,1,4]{0,2,1:T(4,128)}, u32[]{:S(2)}) copy-start(f32[8,1,4]{0,2,1:T(4,128)} %param.13) | copy-start | bytes 388
  0.8 2.2 %copy-start = (bf16[8,1,256,1024]{3,2,1,0:T(8,128)(2,1)S(1)}, bf16[8,1,256,1024]{3,2,1,0:T(8,128)(2,1)}, u32[]{:S(2)}) copy-start(bf16[8,1,256,1024]{3,2,1,0:T(8,128)(2,1)} %param.17) | copy-start | bytes 12582916
  3.0 0.8 %copy-start.4 = (bf16[8,1,4,1024]{3,2,1,0:T(4,128)(2,1)S(1)}, bf16[8,1,4,1024]{3,2,1,0:T(4,128)(2,1)}, u32[]{:S(2)}) copy-start(bf16[8,1,4,1024]{3,2,1,0:T(4,128)(2,1)} %param.10) | copy-start | bytes 196612
  3.8 0.8 %copy-start.6 = (bf16[8,1,4,1024]{3,2,1,0:T(4,128)(2,1)S(1)}, bf16[8,1,4,1024]{3,2,1,0:T(4,128)(2,1)}, u32[]{:S(2)}) copy-start(bf16[8,1,4,1024]{3,2,1,0:T(4,128)(2,1)} %param.11) | copy-start | bytes 196612
  4.6 0.7 %copy-start.9 = (f32[8,1,4]{0,2,1:T(4,128)S(1)}, f32[8,1,4]{0,2,1:T(4,128)}, u32[]{:S(2)}) copy-start(f32[8,1,4]{0,2,1:T(4,128)} %param.13) | copy-start | bytes 388
  5.3 0.7 %copy-start.11 = (f32[8,1,4]{0,2,1:T(4,128)S(1)}, f32[8,1,4]{0,2,1:T(4,128)}, u32[]{:S(2)}) copy-start(f32[8,1,4]{0,2,1:T(4,128)} %param.14) | copy-start | bytes 388
  6.0 11.9 %copy-start.1 = (bf16[8,1,256,1024]{3,2,1,0:T(8,128)(2,1)S(1)}, bf16[8,1,256,1024]{3,2,1,0:T(8,128)(2,1)}, u32[]{:S(2)}) copy-start(bf16[8,1,256,1024]{3,2,1,0:T(8,128)(2,1)} %param.17) | copy-start | bytes 12582916
  6.0 11.9 %copy-start.5 = (bf16[8,1,4,1024]{3,2,1,0:T(4,128)(2,1)S(1)}, bf16[8,1,4,1024]{3,2,1,0:T(4,128)(2,1)}, u32[]{:S(2)}) copy-start(bf16[8,1,4,1024]{3,2,1,0:T(4,128)(2,1)} %param.10) | copy-start | bytes 196612
  6.0 11.9 %copy-start.7 = (bf16[8,1,4,1024]{3,2,1,0:T(4,128)(2,1)S(1)}, bf16[8,1,4,1024]{3,2,1,0:T(4,128)(2,1)}, u32[]{:S(2)}) copy-start(bf16[8,1,4,1024]{3,2,1,0:T(4,128)(2,1)} %param.11) | copy-start | bytes 196612
  6.0 11.9 %copy-start.8 = (bf16[8,1,4,1024]{3,2,1,0:T(4,128)(2,1)S(1)}, bf16[8,1,4,1024]{3,2,1,0:T(4,128)(2,1)}, u32[]{:S(2)}) copy-start(bf16[8,1,4,1024]{3,2,1,0:T(4,128)(2,1)} %param.12) | copy-start | bytes 196612
  17.9 2.2 %copy-start.3 = (bf16[8,1,1024,256]{3,2,1,0:T(8,128)(2,1)S(1)}, bf16[8,1,1024,256]{3,2,1,0:T(8,128)(2,1)}, u32[]{:S(2)}) copy-start(bf16[8,1,1024,256]{3,2,1,0:T(8,128)(2,1)} %param.18) | copy-start | bytes 12582916
  20.1 10.8 %copy-start.2 = (bf16[1,256,8192]{2,1,0:T(8,128)(2,1)S(1)}, bf16[1,256,8192]{2,1,0:T(8,128)(2,1)}, u32[]{:S(2)}) copy-start(bf16[1,256,8192]{2,1,0:T(8,128)(2,1)} %param.19) | copy-start | bytes 12582916
  20.1 10.8 %copy-start.13 = (f32[1,256]{1,0:T(1,128)S(1)}, f32[1,256]{1,0:T(1,128)}, u32[]{:S(2)}) copy-start(f32[1,256]{1,0:T(1,128)} %gain.1) | copy-start | bytes 3076
  23.4 1.3 %collective-permute-start = (bf16[32,1152]{1,0:T(8,128)(2,1)S(1)}, bf16[32,1152]{1,0:T(8,128)(2,1)S(1)}, u32[]{:S(2)}, u32[]{:S(2)}) collective-permute-start(bf16[32,1152]{1,0:T(8,128)(2,1)S(1)} %get-tuple-element.10), channel_id=1, source_target_pairs={{0,32},{32,0},{1,33},{33,1},{2,34},{34,2},{3,35},{35,3},{4,36},{36... | collective-permute-start | bytes 221192 | tf_op jit(solution)/shard_map/ppermute | solution.py:217
  24.8 6.1 %collective-permute-start.1 = (bf16[32,1152]{1,0:T(8,128)(2,1)S(1)}, bf16[32,1152]{1,0:T(8,128)(2,1)S(1)}, u32[]{:S(2)}, u32[]{:S(2)}) collective-permute-start(bf16[32,1152]{1,0:T(8,128)(2,1)S(1)} %add_convert_fusion.mine), channel_id=1, source_target_pairs={{0,64},{64,0},{1,65},{65,1},{2,66},{66,2},{3,67},{67,3},{4,68},{68... | collective-permute-start | bytes 221192 | tf_op jit(solution)/shard_map/ppermute | solution.py:217
  32.3 1.6 %collective-permute-start.2 = (bf16[34,32,128]{2,1,0:T(8,128)(2,1)S(1)}, bf16[34,32,128]{2,1,0:T(8,128)(2,1)S(1)}, u32[]{:S(2)}, u32[]{:S(2)}) collective-permute-start(bf16[34,32,128]{2,1,0:T(8,128)(2,1)S(1)} %get-tuple-element.12), channel_id=1, source_target_pairs={{0,32},{32,0},{1,33},{33,1},{2,34},{34,2},{3,35},{35,3},{4,36},{36... | collective-permute-start | bytes 835592 | tf_op jit(solution)/shard_map/ppermute | solution.py:217

commit v2 on v1

v2 whole, which is shorter than its diff:
```python
import jax
import jax.numpy as jnp
from jax import lax
from jax.experimental import pallas as pl
from jax.experimental.pallas import tpu as pltpu
from jax.sharding import Mesh, PartitionSpec as P

DRAFT = 4
SEQS = 8
ROWS = SEQS * DRAFT
DK = 1024
DV = 1024
PART = 256
HEADS = 16
F32 = jnp.float32
BF16 = jnp.bfloat16
KEY = ("xh", "core")
HBM = pl.BlockSpec(memory_space=pltpu.HBM)
VMEM = pl.BlockSpec(memory_space=pltpu.VMEM)
NT = (((1,), (1,)), ((), ()))
NN = (((1,), (0,)), ((), ()))


def mm(a, b, dims=NN):
    return lax.dot_general(a, b, dims, preferred_element_type=F32)


def halves(x):
    hi = x.astype(BF16)
    return hi, (x - hi.astype(F32)).astype(BF16)


def mm_wide(a, b):
    hi, lo = halves(a)
    return mm(hi, b) + mm(lo, b)


def coefficients(decay, write):
    totals = [decay[0:1]]
    for t in range(1, DRAFT):
        totals.append(totals[-1] * decay[t : t + 1])
    row = lax.broadcasted_iota(jnp.int32, (ROWS, SEQS), 0)
    seq = lax.broadcasted_iota(jnp.int32, (ROWS, SEQS), 1)
    token = row % DRAFT

    def column(rows):
        spread = jnp.zeros((ROWS, SEQS), F32)
        for t in range(DRAFT):
            spread = jnp.where(token == t, jnp.broadcast_to(rows[t], (ROWS, SEQS)), spread)
        return jnp.sum(jnp.where(row // DRAFT == seq, spread, 0.0), axis=1, keepdims=True)

    total = column(totals)
    written = column([write[t : t + 1] for t in range(DRAFT)])
    i = lax.broadcasted_iota(jnp.int32, (ROWS, ROWS), 0)
    j = lax.broadcasted_iota(jnp.int32, (ROWS, ROWS), 1)

    def as_row(col):
        return jnp.sum(jnp.where(i == j, jnp.broadcast_to(col, (ROWS, ROWS)), 0.0), axis=0, keepdims=True)

    kept = (i // DRAFT == j // DRAFT) & (j <= i)
    mix = jnp.where(kept, as_row(written) * (total / as_row(total)), 0.0)
    return total, mix


def stack(ref, out):
    for s in range(SEQS):
        out[DRAFT * s : DRAFT * (s + 1), :] = ref[s].astype(F32)


def position():
    xh, core = lax.axis_index("xh"), lax.axis_index("core")
    return 2 * xh + core, core, xh


def first_kernel(
    q_hbm, k_hbm, v_hbm, decay_hbm, write_hbm, cov_hbm, val_hbm,
    msg, cov, val, q32, k32, v_mine, total_out, mix_out,
    q_in, k_in, v_in, decay_in, write_in, z32, small_sem, big_sem,
):
    start = pl.multiple_of(position()[0] * PART, PART)
    ends = [
        (decay_hbm, decay_in),
        (write_hbm, write_in),
        (q_hbm, q_in),
        (k_hbm, k_in),
        (v_hbm.at[:, :, pl.ds(start, PART)], v_in),
    ]
    small = [pltpu.make_async_copy(a, b, small_sem.at[n]) for n, (a, b) in enumerate(ends)]
    big = [
        pltpu.make_async_copy(cov_hbm.at[pl.ds(2 * p, 2)], cov.at[pl.ds(2 * p, 2)], big_sem.at[p])
        for p in range(SEQS // 2)
    ]
    big.append(pltpu.make_async_copy(val_hbm, val, big_sem.at[SEQS // 2]))
    for c in small + big[:1]:
        c.start()
    for c in small[:2]:
        c.wait()
    big[1].start()
    big[2].start()
    total, mix = coefficients(decay_in[...], write_in[...])
    total_out[...] = jnp.broadcast_to(total, total_out.shape)
    mix_out[...] = mix
    for c, x, out in zip(small[2:], (q_in, k_in, v_in), (q32, k32, v_mine)):
        c.wait()
        stack(x, out)
    keys = k32[...].astype(BF16)
    keys_mine = k32[:, pl.ds(start, PART)].astype(BF16)
    dots = mm(q32[...].astype(BF16), keys, NT)
    base = mm_wide(mix * dots, keys_mine)
    first = lax.broadcasted_iota(jnp.int32, (8, 1), 0) < DRAFT

    def by_columns(p, pieces):
        both = jnp.concatenate(pieces, axis=0)
        res = [mm(both, cov[2 * p + n]) for n in range(2)]
        z = jnp.where(first, res[0][:8] + res[0][8:], res[1][:8] + res[1][8:])
        z32[8 * p : 8 * p + 8, :] = z * total[8 * p : 8 * p + 8]

    held = None
    for p in range(SEQS // 2):
        big[p].wait()
        if p == 0:
            big[3].start()
            big[4].start()
        slab = q32[8 * p : 8 * p + 8, :].astype(BF16)
        res = [mm(slab, cov[2 * p + n], NT) for n in range(2)]
        y = jnp.where(first, res[0], res[1]) * total[8 * p : 8 * p + 8] + base[8 * p : 8 * p + 8]
        pieces = halves(y)
        msg[8 * p : 8 * p + 8, DK : DK + PART] = pieces[0]
        msg[8 * p : 8 * p + 8, DK + PART :] = pieces[1]
        if held is not None:
            by_columns(*held)
        held = (p, pieces)
    by_columns(*held)
    y_hi, y_lo = msg[:, DK : DK + PART], msg[:, DK + PART :]
    dots = mm(y_hi, keys_mine, NT) + mm(y_lo, keys_mine, NT)
    msg[:, :DK] = (z32[...] + mm_wide(mix * dots, keys)).astype(BF16)
    big[4].wait()


def second_kernel(
    ridge, gathered, cov, val, q32, k32, v_mine, total_in, mix_in, sent, kept,
    y32, w32, d32, x32, aw32, r1, r2, l1, l2,
):
    total, shift, mix = total_in[:, :1], ridge[0:1, 0:1], mix_in[...]
    me, core, _ = position()
    mine = pl.ds(pl.multiple_of(me * PART, PART), PART)
    first = lax.broadcasted_iota(jnp.int32, (8, 1), 0) < DRAFT

    def dot(a, b):
        return jnp.sum(a * b, axis=1, keepdims=True)

    for g in range(4):
        y32[:, g * PART : (g + 1) * PART] = gathered[g, :, DK : DK + PART].astype(F32) + gathered[
            g, :, DK + PART :
        ].astype(F32)
    w = y32[...]
    y32[...] = w + shift * q32[...]
    w = shift * (w + y32[...])
    for g in range(4):
        w = w + gathered[g, :, :DK].astype(F32)
    w32[...] = w
    keys = k32[...].astype(BF16)
    keys_mine = k32[:, mine].astype(BF16)
    for p in range(SEQS // 2):
        rows = slice(8 * p, 8 * p + 8)
        lhs = jnp.concatenate(halves(w32[rows, :]), axis=0)
        res = [mm(lhs, cov[2 * p + n], NT) for n in range(2)]
        aw32[rows, :] = jnp.where(first, res[0][:8] + res[0][8:], res[1][:8] + res[1][8:]) * total[rows]
    dots_w = mm(jnp.concatenate(halves(w32[...]), axis=0), keys, NT)
    image_w = aw32[...] + mm_wide(mix * (dots_w[:ROWS] + dots_w[ROWS:]), keys_mine) + shift * w32[:, mine]

    q, y, w = q32[...], y32[...], w32[...]
    rr0 = dot(q, q)
    a0 = rr0 / dot(q, y)
    res1 = q - a0 * y
    rr1 = dot(res1, res1)
    b0 = rr1 / rr0
    dir1 = res1 + b0 * q
    image1 = (1.0 + b0) * y - a0 * w
    a1 = rr1 / dot(dir1, image1)
    sol2 = a0 * q + a1 * dir1
    res2 = res1 - a1 * image1
    rr2 = dot(res2, res2)
    b1 = rr2 / rr1
    dir2 = res2 + b1 * dir1
    d32[...] = dir2
    x32[...] = sol2
    y, w = y32[:, mine], w32[:, mine]
    image2 = y - a0 * w - a1 * ((1.0 + b0) * w - a0 * image_w) + b1 * ((1.0 + b0) * y - a0 * w)
    share = jnp.broadcast_to(dot(d32[:, mine], image2) / rr2, (ROWS, 128))
    dots = mm(jnp.concatenate(halves(sol2) + (dir2.astype(BF16),), axis=0), keys, NT)
    values = v_mine[...].astype(BF16)
    l1[...] = mm_wide(mix * (dots[:ROWS] + dots[ROWS : 2 * ROWS]), values)
    l2[...] = mm_wide(mix * dots[2 * ROWS :], values)
    for out in (sent, kept):
        out[:, 4 * PART :] = share.astype(out.dtype)
    for p in range(SEQS // 2):
        rows = slice(8 * p, 8 * p + 8)
        lhs = jnp.concatenate([x32[rows, mine].astype(BF16), d32[rows, mine].astype(BF16)], axis=0)
        res = [mm(lhs, val[2 * p + n], NT) for n in range(2)]
        r1[rows, :] = jnp.where(first, res[0][:8], res[1][:8]) * total[rows]
        r2[rows, :] = jnp.where(first, res[0][8:], res[1][8:]) * total[rows]
        r1[rows, mine] += l1[rows, :]
        r2[rows, mine] += l2[rows, :]
        for out, c in ((sent, 1 - core), (kept, core)):
            for x in range(2):
                cols = pl.ds(pl.multiple_of((2 * x + c) * PART, PART), PART)
                out[rows, x * PART : (x + 1) * PART] = r1[rows, cols].astype(out.dtype)
                out[rows, (2 + x) * PART : (3 + x) * PART] = r2[rows, cols].astype(out.dtype)


def third_kernel(mine, arrived, gain, weight, sent, kept):
    _, core, xh = position()
    total = mine[...].astype(F32) + arrived[...].astype(F32)
    a2 = 1.0 / total[:, 4 * PART : 4 * PART + 1]
    readout = total[:, : 2 * PART] + a2 * total[:, 2 * PART : 4 * PART]
    squares = jnp.broadcast_to(jnp.sum(readout * readout, axis=1, keepdims=True), (ROWS, 128))
    own = jnp.where(xh == 0, readout[:, :PART], readout[:, PART:])
    scaled = (own * gain[...]).astype(BF16)
    step = 512
    for out, c in ((sent, 1 - core), (kept, core)):
        for x in range(2):
            for n in range(2048 // step):
                cols = pl.ds(pl.multiple_of((2 * x + c) * 2048 + n * step, step), step)
                part = mm(scaled, weight[:, cols])
                for m in range(step // 128):
                    out[16 * x + n * (step // 128) + m] = part[:, 128 * m : 128 * (m + 1)].astype(out.dtype)
        hi, lo = halves(squares)
        out[32] = hi.astype(out.dtype)
        out[33] = lo.astype(out.dtype)


def swapped(x, axis):
    return lax.ppermute(x, axis, [(0, 1), (1, 0)])


def params(mib):
    return pltpu.CompilerParams(vmem_limit_bytes=mib << 20)


def body(
    new_queries, new_keys, new_values, decay_gate, write_gate,
    ridge_shift, norm_gain, cov_state, value_state, out_weight,
):
    q, k, v = (x[:, 0] for x in (new_queries, new_keys, new_values))
    decay, write = (x[:, 0].T for x in (decay_gate, write_gate))
    cov, val, weight = cov_state[:, 0], value_state[:, 0], out_weight[0]

    in_hbm = [
        pltpu.with_memory_space_constraint(x, pltpu.HBM)
        for x in (q, k, v, decay, write, cov, val)
    ]
    msg, *carried = pl.pallas_call(
        first_kernel,
        name="first",
        out_shape=(
            pltpu.VMEM((ROWS, DK + 2 * PART), BF16),
            pltpu.VMEM((SEQS, PART, DK), BF16),
            pltpu.VMEM((SEQS, DV, PART), BF16),
            pltpu.VMEM((ROWS, DK), F32),
            pltpu.VMEM((ROWS, DK), F32),
            pltpu.VMEM((ROWS, PART), F32),
            pltpu.VMEM((ROWS, 128), F32),
            pltpu.VMEM((ROWS, ROWS), F32),
        ),
        in_specs=[HBM] * 7,
        out_specs=(VMEM,) * 8,
        scratch_shapes=[
            pltpu.VMEM((SEQS, DRAFT, DK), BF16),
            pltpu.VMEM((SEQS, DRAFT, DK), BF16),
            pltpu.VMEM((SEQS, DRAFT, PART), BF16),
            pltpu.VMEM((DRAFT, SEQS), F32),
            pltpu.VMEM((DRAFT, SEQS), F32),
            pltpu.VMEM((ROWS, DK), F32),
            pltpu.SemaphoreType.DMA((5,)),
            pltpu.SemaphoreType.DMA((SEQS // 2 + 1,)),
        ],
        compiler_params=params(16),
    )(*in_hbm)
    gathered = lax.all_gather(msg, KEY)
    sent, kept = pl.pallas_call(
        second_kernel,
        name="second",
        out_shape=(
            jax.ShapeDtypeStruct((ROWS, 4 * PART + 128), BF16),
            jax.ShapeDtypeStruct((ROWS, 4 * PART + 128), F32),
        ),
        in_specs=[VMEM] * 9,
        out_specs=(VMEM, VMEM),
        scratch_shapes=[pltpu.VMEM((ROWS, n), F32) for n in (DK, DK, DK, DK, PART, DV, DV, PART, PART)],
        compiler_params=params(16),
    )(jnp.broadcast_to(ridge_shift[None], (8, 128)), gathered, *carried)
    pair = (kept + swapped(sent, "core").astype(F32)).astype(BF16)
    other = swapped(pair, "xh")
    sent, kept = pl.pallas_call(
        third_kernel,
        name="third",
        out_shape=(
            jax.ShapeDtypeStruct((34, ROWS, 128), BF16),
            jax.ShapeDtypeStruct((34, ROWS, 128), F32),
        ),
        in_specs=[VMEM] * 4,
        out_specs=(VMEM, VMEM),
        compiler_params=params(16),
    )(pair, other, norm_gain, weight)
    arrived = swapped(sent, "core").astype(F32)
    squares = kept[32] + kept[33] + arrived[32] + arrived[33]
    scale = lax.rsqrt(squares * (1.0 / DV) + 1e-06)
    part = ((kept[:32] + arrived[:32]) * scale).astype(BF16)
    landed = lax.all_to_all(part, ("xh", "head"), 0, 0, tiled=True)
    out = landed.astype(F32).sum(axis=0).astype(BF16)
    return out.reshape(SEQS, DRAFT, 128)


def solution(mesh):
    fine = Mesh(mesh.devices.reshape(2, 2, *mesh.devices.shape[1:]), ("xh", "core", "head", "batch"))
    placed = (
        P("batch", "head", None, None),
        P("batch", "head", None, None),
        P("batch", "head", None, None),
        P("batch", "head", None),
        P("batch", "head", None),
        P("head"),
        P("head", KEY),
        P("batch", "head", KEY, None),
        P("batch", "head", None, KEY),
        P("head", KEY, None),
    )
    return jax.shard_map(
        body,
        mesh=fine,
        in_specs=placed,
        out_specs=P("batch", None, ("xh", "core", "head")),
        check_vma=False,
    )
```

time: 56.2 us -> 47.9 us (0.85)
  local copies, waits for them, and re-layouts: 7.44 us -> 0.01 us
  Pallas kernels: 8.46 us -> 7.88 us
    unnamed x28 -> x4, local copies, waits for them, and re-layouts: 7.44 us -> 0.01 us
where the time goes in v2:
time: 47.9 us; the launch traced here: 47.7 us
  blocking collectives  29.2 us (61%)
  Pallas kernels  7.88 us (16%)
  waiting for transfers between devices  5.81 us (12%)
  starting transfers between devices  3.24 us (7%)
  other arithmetic  0.85 us (2%)
  between operations  0.7 us (1%)
    all_to_all x1, blocking collectives, body(): landed = lax.all_to_all(part, ('xh', 'head'), 0, 0, tiled=True)  21.1 us
    all_gather x1, blocking collectives, body(): gathered = lax.all_gather(msg, KEY)  8.1 us
    ppermute x3, waiting for transfers between devices, swapped(): return lax.ppermute(x, axis, [(0, 1), (1, 0)])  5.81 us
    pallas_call x1, Pallas kernels, body(): pl.pallas_call(first_kernel, name='first', out_shape=(pltpu.VMEM((ROWS, D...  4.17 us
    ppermute x3, starting transfers between devices, swapped(): return lax.ppermute(x, axis, [(0, 1), (1, 0)])  3.24 us
    pallas_call x1, Pallas kernels, body(): pl.pallas_call(second_kernel, name='second', out_shape=(jax.ShapeDtypeStr...  2.83 us
  transfers between devices with their start and end apart: 3, of which 3 were waited for; matrix products, arithmetic and copies ran while one was open for 0% of the time, Pallas kernels for 0%

profile of v2, /device:TPU:0, one launch (start us, length us, event | category | flops | bytes accessed | tf_op | source)
XLA Modules:
  0.0 47.7 jit_solution(4962107555754213710)
XLA Ops:
  0.7 4.2 %first.1 = (bf16[32,1536]{1,0:T(8,128)(2,1)S(1)}, bf16[8,256,1024]{2,1,0:T(8,128)(2,1)S(1)}, bf16[8,1024,256]{2,1,0:T(8,128)(2,1)S(1)}, f32[32,1024]{1,0:T(8,128...) custom-call(bf16[8,4,1024]{2,1,0:T(4,128)(2,1)} %bitcast.22, ...), custom_call_target="tpu_custom_call" | custom-call | tf_op jit(solution)/shard_map/first/pallas_call | solution.py:253
  4.8 8.1 %all-gather = bf16[128,1536]{1,0:T(8,128)(2,1)S(1)} all-gather(bf16[32,1536]{1,0:T(8,128)(2,1)S(1)} %get-tuple-element.17), channel_id=2, replica_groups=mesh['xh'=2,'core'=2,'head'=16,'batch'=2] {'xh','core'}, dimensions={0}, use_global_device_ids=true | all-gather | bytes 491520 | tf_op jit(solution)/shard_map/all_gather | solution.py:280
  12.9 0.0 copy-start
  12.9 0.0 copy-start.1
  12.9 2.8 %second.1 = (bf16[32,1152]{1,0:T(8,128)(2,1)S(1)}, f32[32,1152]{1,0:T(8,128)S(1)}) custom-call(f32[8,128]{1,0:T(8,128)S(1)} %broadcast_in_dim.10.ridge, bf16[4,32,1536]{2,1,0:T(8,128)(2,1)S(1)} %bitcast.19, bf16[8,256,1024]{2,1,0:T(8,128)(2,1)S(1)} %get-tuple-element.18.cov, bf16[8,1024,256]{2,1,0:T(8,128)(2,1)S(1)} %get-tuple-element.19.val, ...), custom_call_target="tpu_custom_call" | custom-call | tf_op jit(solution)/shard_map/second/pallas_call | solution.py:281
  15.8 0.4 collective-permute-start
  16.2 0.9 %collective-permute-done = bf16[32,1152]{1,0:T(8,128)(2,1)S(1)} collective-permute-done((bf16[32,1152]{1,0:T(8,128)(2,1)S(1)}, bf16[32,1152]{1,0:T(8,128)(2,1)S(1)}, u32[]{:S(2)}, u32[]{:S(2)}) %collective-permute-start) | collective-permute-done | bytes 73760 | tf_op jit(solution)/shard_map/ppermute | solution.py:234
  17.1 2.8 %collective-permute-start.1 = (bf16[32,1152]{1,0:T(8,128)(2,1)S(1)}, bf16[32,1152]{1,0:T(8,128)(2,1)S(1)}, u32[]{:S(2)}, u32[]{:S(2)}) collective-permute-start(bf16[32,1152]{1,0:T(8,128)(2,1)S(1)} %add_convert_fusion.mine), channel_id=1, source_target_pairs={{0,64},{64,0},{1,65},{65,1},{2,66},{66,2},{3,67},{67,3},{4,68},{68... | collective-permute-start | bytes 221192 | tf_op jit(solution)/shard_map/ppermute | solution.py:234
  19.9 3.4 %collective-permute-done.1.arrived = bf16[32,1152]{1,0:T(8,128)(2,1)S(1)} collective-permute-done((bf16[32,1152]{1,0:T(8,128)(2,1)S(1)}, bf16[32,1152]{1,0:T(8,128)(2,1)S(1)}, u32[]{:S(2)}, u32[]{:S(2)}) %collective-permute-start.1) | collective-permute-done | bytes 73760 | tf_op jit(solution)/shard_map/ppermute | solution.py:234
  23.3 0.0 copy-done
  23.3 0.0 copy-done.1
  23.3 0.9 %third.1 = (bf16[34,32,128]{2,1,0:T(8,128)(2,1)S(1)}, f32[34,32,128]{2,1,0:T(8,128)S(1)}) custom-call(bf16[32,1152]{1,0:T(8,128)(2,1)S(1)} %add_convert_fusion.mine, bf16[32,1152]{1,0:T(8,128)(2,1)S(1)} %collective-permute-done.1.arrived, f32[1,256]{1,0:T(1,128)S(1)} %copy-done.1, bf16[256,8192]{1,0:T(8,128)(2,1)S(1)} %bitcast.18), custom_call_target="tpu_custom_call" | custom-call | tf_op jit(solution)/shard_map/third/pallas_call | solution.py:295
  24.1 0.1 collective-permute-start.2
  24.2 1.5 %collective-permute-done.2 = bf16[34,32,128]{2,1,0:T(8,128)(2,1)S(1)} collective-permute-done((bf16[34,32,128]{2,1,0:T(8,128)(2,1)S(1)}, bf16[34,32,128]{2,1,0:T(8,128)(2,1)S(1)}, u32[]{:S(2)}, u32[]{:S(2)}) %collective-permute-start.2) | collective-permute-done | bytes 278560 | tf_op jit(solution)/shard_map/ppermute | solution.py:234
  25.8 0.1 convert_element_type.16
  25.8 0.1 fusion.1
  26.0 21.1 %all_to_all.5 = bf16[32,32,128]{2,1,0:T(8,128)(2,1)S(1)} all-to-all(bf16[32,32,128]{2,1,0:T(8,128)(2,1)S(1)} %fusion.1), channel_id=1, replica_groups=mesh['xh'=2,'core'=2,'head'=16,'batch'=2] {'xh','head'}, dimensions={0} | all-to-all | bytes 524288 | tf_op jit(solution)/shard_map/all_to_all | solution.py:310
  47.1 0.6 %reduce_sum.12 = bf16[32,128]{1,0:T(8,128)(2,1)} reduce(bf16[32,32,128]{2,1,0:T(8,128)(2,1)S(1)} %all_to_all.5, bf16[]{:T(256)} %constant.6.clone.1), dimensions={0}, to_apply=%region_0.0 | reduce | flops 126976 | bytes 270338 | tf_op jit(solution)/shard_map/reduce_sum | solution.py:311
  (3 shorter events, 0.0 us)
Async XLA Ops:
  12.9 10.3 %copy-start = (bf16[1,256,8192]{2,1,0:T(8,128)(2,1)S(1)}, bf16[1,256,8192]{2,1,0:T(8,128)(2,1)}, u32[]{:S(2)}) copy-start(bf16[1,256,8192]{2,1,0:T(8,128)(2,1)} %param.19) | copy-start | bytes 12582916
  12.9 10.3 %copy-start.1 = (f32[1,256]{1,0:T(1,128)S(1)}, f32[1,256]{1,0:T(1,128)}, u32[]{:S(2)}) copy-start(f32[1,256]{1,0:T(1,128)} %gain.1) | copy-start | bytes 3076
  15.8 1.3 %collective-permute-start = (bf16[32,1152]{1,0:T(8,128)(2,1)S(1)}, bf16[32,1152]{1,0:T(8,128)(2,1)S(1)}, u32[]{:S(2)}, u32[]{:S(2)}) collective-permute-start(bf16[32,1152]{1,0:T(8,128)(2,1)S(1)} %get-tuple-element.26), channel_id=1, source_target_pairs={{0,32},{32,0},{1,33},{33,1},{2,34},{34,2},{3,35},{35,3},{4,36},{36... | collective-permute-start | bytes 221192 | tf_op jit(solution)/shard_map/ppermute | solution.py:234
  17.1 6.1 %collective-permute-start.1 = (bf16[32,1152]{1,0:T(8,128)(2,1)S(1)}, bf16[32,1152]{1,0:T(8,128)(2,1)S(1)}, u32[]{:S(2)}, u32[]{:S(2)}) collective-permute-start(bf16[32,1152]{1,0:T(8,128)(2,1)S(1)} %add_convert_fusion.mine), channel_id=1, source_target_pairs={{0,64},{64,0},{1,65},{65,1},{2,66},{66,2},{3,67},{67,3},{4,68},{68... | collective-permute-start | bytes 221192 | tf_op jit(solution)/shard_map/ppermute | solution.py:234
  24.1 1.6 %collective-permute-start.2 = (bf16[34,32,128]{2,1,0:T(8,128)(2,1)S(1)}, bf16[34,32,128]{2,1,0:T(8,128)(2,1)S(1)}, u32[]{:S(2)}, u32[]{:S(2)}) collective-permute-start(bf16[34,32,128]{2,1,0:T(8,128)(2,1)S(1)} %get-tuple-element.28), channel_id=1, source_target_pairs={{0,32},{32,0},{1,33},{33,1},{2,34},{34,2},{3,35},{35,3},{4,36},{36... | collective-permute-start | bytes 835592 | tf_op jit(solution)/shard_map/ppermute | solution.py:234

commit v3 on v2

--- a/solution.py
+++ b/solution.py
@@ -11,6 +11,7 @@
 DK = 1024
 DV = 1024
 PART = 256
+BLOCKS = DK // PART
 HEADS = 16
 F32 = jnp.float32
 BF16 = jnp.bfloat16
@@ -35,6 +36,10 @@
     return mm(hi, b) + mm(lo, b)
 
 
+def by_rows(a, cov, s):
+    return sum(mm(a[:, PART * b : PART * (b + 1)], cov[s, b], NT) for b in range(BLOCKS))
+
+
 def coefficients(decay, write):
     totals = [decay[0:1]]
     for t in range(1, DRAFT):
@@ -75,7 +80,7 @@
 def first_kernel(
     q_hbm, k_hbm, v_hbm, decay_hbm, write_hbm, cov_hbm, val_hbm,
     msg, cov, val, q32, k32, v_mine, total_out, mix_out,
-    q_in, k_in, v_in, decay_in, write_in, z32, small_sem, big_sem,
+    q_in, k_in, v_in, decay_in, write_in, z32, small_sem, big_sem, val_sem,
 ):
     start = pl.multiple_of(position()[0] * PART, PART)
     ends = [
@@ -87,16 +92,21 @@
     ]
     small = [pltpu.make_async_copy(a, b, small_sem.at[n]) for n, (a, b) in enumerate(ends)]
     big = [
-        pltpu.make_async_copy(cov_hbm.at[pl.ds(2 * p, 2)], cov.at[pl.ds(2 * p, 2)], big_sem.at[p])
+        [
+            pltpu.make_async_copy(
+                cov_hbm.at[pl.ds(2 * p, 2), :, pl.ds(PART * b, PART)],
+                cov.at[pl.ds(2 * p, 2), b],
+                big_sem.at[p, b],
+            )
+            for b in range(BLOCKS)
+        ]
         for p in range(SEQS // 2)
     ]
-    big.append(pltpu.make_async_copy(val_hbm, val, big_sem.at[SEQS // 2]))
-    for c in small + big[:1]:
+    big.append([pltpu.make_async_copy(val_hbm, val, val_sem)])
+    for c in small + big[0] + big[1] + big[2] + big[3]:
         c.start()
     for c in small[:2]:
         c.wait()
-    big[1].start()
-    big[2].start()
     total, mix = coefficients(decay_in[...], write_in[...])
     total_out[...] = jnp.broadcast_to(total, total_out.shape)
     mix_out[...] = mix
@@ -111,18 +121,19 @@
 
     def by_columns(p, pieces):
         both = jnp.concatenate(pieces, axis=0)
-        res = [mm(both, cov[2 * p + n]) for n in range(2)]
+        res = [jnp.concatenate([mm(both, cov[2 * p + n, b]) for b in range(BLOCKS)], axis=1) for n in range(2)]
         z = jnp.where(first, res[0][:8] + res[0][8:], res[1][:8] + res[1][8:])
         z32[8 * p : 8 * p + 8, :] = z * total[8 * p : 8 * p + 8]
 
     held = None
     for p in range(SEQS // 2):
-        big[p].wait()
+        for c in big[p]:
+            c.wait()
         if p == 0:
-            big[3].start()
-            big[4].start()
+            for c in big[4]:
+                c.start()
         slab = q32[8 * p : 8 * p + 8, :].astype(BF16)
-        res = [mm(slab, cov[2 * p + n], NT) for n in range(2)]
+        res = [by_rows(slab, cov, 2 * p + n) for n in range(2)]
         y = jnp.where(first, res[0], res[1]) * total[8 * p : 8 * p + 8] + base[8 * p : 8 * p + 8]
         pieces = halves(y)
         msg[8 * p : 8 * p + 8, DK : DK + PART] = pieces[0]
@@ -130,16 +141,17 @@
         if held is not None:
             by_columns(*held)
         held = (p, pieces)
-    by_columns(*held)
     y_hi, y_lo = msg[:, DK : DK + PART], msg[:, DK + PART :]
     dots = mm(y_hi, keys_mine, NT) + mm(y_lo, keys_mine, NT)
-    msg[:, :DK] = (z32[...] + mm_wide(mix * dots, keys)).astype(BF16)
-    big[4].wait()
+    low_rank = mm_wide(mix * dots, keys)
+    by_columns(*held)
+    msg[:, :DK] = (z32[...] + low_rank).astype(BF16)
+    big[4][0].wait()
 
 
 def second_kernel(
-    ridge, gathered, cov, val, q32, k32, v_mine, total_in, mix_in, sent, kept,
-    y32, w32, d32, x32, aw32, r1, r2, l1, l2,
+    ridge, gathered, cov, val, q32, k32, v_mine, total_in, mix_in, sent, lhs, low, share_out,
+    y32, w32, d32, x32, aw32,
 ):
     total, shift, mix = total_in[:, :1], ridge[0:1, 0:1], mix_in[...]
     me, core, _ = position()
@@ -163,8 +175,8 @@
     keys_mine = k32[:, mine].astype(BF16)
     for p in range(SEQS // 2):
         rows = slice(8 * p, 8 * p + 8)
-        lhs = jnp.concatenate(halves(w32[rows, :]), axis=0)
-        res = [mm(lhs, cov[2 * p + n], NT) for n in range(2)]
+        pieces = jnp.concatenate(halves(w32[rows, :]), axis=0)
+        res = [by_rows(pieces, cov, 2 * p + n) for n in range(2)]
         aw32[rows, :] = jnp.where(first, res[0][:8] + res[0][8:], res[1][:8] + res[1][8:]) * total[rows]
     dots_w = mm(jnp.concatenate(halves(w32[...]), axis=0), keys, NT)
     image_w = aw32[...] + mm_wide(mix * (dots_w[:ROWS] + dots_w[ROWS:]), keys_mine) + shift * w32[:, mine]
@@ -188,46 +200,67 @@
     y, w = y32[:, mine], w32[:, mine]
     image2 = y - a0 * w - a1 * ((1.0 + b0) * w - a0 * image_w) + b1 * ((1.0 + b0) * y - a0 * w)
     share = jnp.broadcast_to(dot(d32[:, mine], image2) / rr2, (ROWS, 128))
-    dots = mm(jnp.concatenate(halves(sol2) + (dir2.astype(BF16),), axis=0), keys, NT)
-    values = v_mine[...].astype(BF16)
-    l1[...] = mm_wide(mix * (dots[:ROWS] + dots[ROWS : 2 * ROWS]), values)
-    l2[...] = mm_wide(mix * dots[2 * ROWS :], values)
-    for out in (sent, kept):
-        out[:, 4 * PART :] = share.astype(out.dtype)
+    sent[:, 4 * PART :] = share.astype(BF16)
+    share_out[...] = share
     for p in range(SEQS // 2):
         rows = slice(8 * p, 8 * p + 8)
-        lhs = jnp.concatenate([x32[rows, mine].astype(BF16), d32[rows, mine].astype(BF16)], axis=0)
-        res = [mm(lhs, val[2 * p + n], NT) for n in range(2)]
-        r1[rows, :] = jnp.where(first, res[0][:8], res[1][:8]) * total[rows]
-        r2[rows, :] = jnp.where(first, res[0][8:], res[1][8:]) * total[rows]
-        r1[rows, mine] += l1[rows, :]
-        r2[rows, mine] += l2[rows, :]
-        for out, c in ((sent, 1 - core), (kept, core)):
-            for x in range(2):
-                cols = pl.ds(pl.multiple_of((2 * x + c) * PART, PART), PART)
-                out[rows, x * PART : (x + 1) * PART] = r1[rows, cols].astype(out.dtype)
-                out[rows, (2 + x) * PART : (3 + x) * PART] = r2[rows, cols].astype(out.dtype)
-
-
-def third_kernel(mine, arrived, gain, weight, sent, kept):
+        both = [x32[rows, mine].astype(BF16), d32[rows, mine].astype(BF16)]
+        lhs[2 * 8 * p : 2 * 8 * (p + 1), :] = jnp.concatenate(both, axis=0)
+        if p == 2:
+            dots = mm(jnp.concatenate(halves(x32[...]) + (d32[...].astype(BF16),), axis=0), keys, NT)
+        by_values(lhs, val, total, 1 - core, p, sent)
+    values = v_mine[...].astype(BF16)
+    low[:, :PART] = mm_wide(mix * (dots[:ROWS] + dots[ROWS : 2 * ROWS]), values)
+    low[:, PART:] = mm_wide(mix * dots[2 * ROWS :], values)
+
+
+def by_values(lhs, val, total, core, p, out):
+    rows = slice(8 * p, 8 * p + 8)
+    first = lax.broadcasted_iota(jnp.int32, (8, 1), 0) < DRAFT
+    both = lhs[16 * p : 16 * p + 16, :]
+    for x in range(2):
+        entries = pl.ds(pl.multiple_of((2 * x + core) * PART, PART), PART)
+        res = [mm(both, val[2 * p + n, entries, :], NT) for n in range(2)]
+        for m in range(2):
+            half = slice(8 * m, 8 * m + 8)
+            part = jnp.where(first, res[0][half], res[1][half]) * total[rows]
+            out[rows, (2 * m + x) * PART : (2 * m + x + 1) * PART] = part.astype(out.dtype)
+
+
+def own_kernel(val, lhs, total_in, low, share, kept):
+    _, core, xh = position()
+    total = total_in[:, :1]
+    for p in range(SEQS // 2):
+        by_values(lhs, val, total, core, p, kept)
+    kept[:, 4 * PART :] = share[...]
+    for m in range(2):
+        kept[:, pl.ds(pl.multiple_of((2 * m + xh) * PART, PART), PART)] += low[:, m * PART : (m + 1) * PART]
+
+
+def project(scaled, weight, core, out):
+    step = 512
+    for x in range(2):
+        for n in range(2048 // step):
+            cols = pl.ds(pl.multiple_of((2 * x + core) * 2048 + n * step, step), step)
+            part = mm(scaled, weight[:, cols])
+            for m in range(step // 128):
+                out[16 * x + n * (step // 128) + m] = part[:, 128 * m : 128 * (m + 1)].astype(out.dtype)
+
+
+def third_kernel(mine, arrived, gain, weight, sent, scaled, squares):
     _, core, xh = position()
     total = mine[...].astype(F32) + arrived[...].astype(F32)
     a2 = 1.0 / total[:, 4 * PART : 4 * PART + 1]
     readout = total[:, : 2 * PART] + a2 * total[:, 2 * PART : 4 * PART]
-    squares = jnp.broadcast_to(jnp.sum(readout * readout, axis=1, keepdims=True), (ROWS, 128))
     own = jnp.where(xh == 0, readout[:, :PART], readout[:, PART:])
-    scaled = (own * gain[...]).astype(BF16)
-    step = 512
-    for out, c in ((sent, 1 - core), (kept, core)):
-        for x in range(2):
-            for n in range(2048 // step):
-                cols = pl.ds(pl.multiple_of((2 * x + c) * 2048 + n * step, step), step)
-                part = mm(scaled, weight[:, cols])
-                for m in range(step // 128):
-                    out[16 * x + n * (step // 128) + m] = part[:, 128 * m : 128 * (m + 1)].astype(out.dtype)
-        hi, lo = halves(squares)
-        out[32] = hi.astype(out.dtype)
-        out[33] = lo.astype(out.dtype)
+    scaled[...] = (own * gain[...]).astype(BF16)
+    project(scaled[...], weight, 1 - core, sent)
+    squares[...] = jnp.broadcast_to(jnp.sum(readout * readout, axis=1, keepdims=True), (ROWS, 128))
+    sent[32], sent[33] = halves(squares[...])
+
+
+def last_kernel(scaled, weight, kept):
+    project(scaled[...], weight, position()[1], kept)
 
 
 def swapped(x, axis):
@@ -246,6 +279,7 @@
     decay, write = (x[:, 0].T for x in (decay_gate, write_gate))
     cov, val, weight = cov_state[:, 0], value_state[:, 0], out_weight[0]
 
+    estimate = pl.CostEstimate(flops=1 << 28, bytes_accessed=1 << 21, transcendentals=0)
     in_hbm = [
         pltpu.with_memory_space_constraint(x, pltpu.HBM)
         for x in (q, k, v, decay, write, cov, val)
@@ -255,7 +289,7 @@
         name="first",
         out_shape=(
             pltpu.VMEM((ROWS, DK + 2 * PART), BF16),
-            pltpu.VMEM((SEQS, PART, DK), BF16),
+            pltpu.VMEM((SEQS, BLOCKS, PART, PART), BF16),
             pltpu.VMEM((SEQS, DV, PART), BF16),
             pltpu.VMEM((ROWS, DK), F32),
             pltpu.VMEM((ROWS, DK), F32),
@@ -273,40 +307,61 @@
             pltpu.VMEM((DRAFT, SEQS), F32),
             pltpu.VMEM((ROWS, DK), F32),
             pltpu.SemaphoreType.DMA((5,)),
-            pltpu.SemaphoreType.DMA((SEQS // 2 + 1,)),
+            pltpu.SemaphoreType.DMA((SEQS // 2, BLOCKS)),
+            pltpu.SemaphoreType.DMA,
         ],
         compiler_params=params(16),
     )(*in_hbm)
     gathered = lax.all_gather(msg, KEY)
-    sent, kept = pl.pallas_call(
+    sent, lhs, low, share = pl.pallas_call(
         second_kernel,
         name="second",
         out_shape=(
-            jax.ShapeDtypeStruct((ROWS, 4 * PART + 128), BF16),
-            jax.ShapeDtypeStruct((ROWS, 4 * PART + 128), F32),
+            pltpu.VMEM((ROWS, 4 * PART + 128), BF16),
+            pltpu.VMEM((2 * ROWS, PART), BF16),
+            pltpu.VMEM((ROWS, 2 * PART), F32),
+            pltpu.VMEM((ROWS, 128), F32),
         ),
         in_specs=[VMEM] * 9,
-        out_specs=(VMEM, VMEM),
-        scratch_shapes=[pltpu.VMEM((ROWS, n), F32) for n in (DK, DK, DK, DK, PART, DV, DV, PART, PART)],
+        out_specs=(VMEM,) * 4,
+        scratch_shapes=[pltpu.VMEM((ROWS, n), F32) for n in (DK, DK, DK, DK, PART)],
         compiler_params=params(16),
     )(jnp.broadcast_to(ridge_shift[None], (8, 128)), gathered, *carried)
+    kept = pl.pallas_call(
+        own_kernel,
+        name="own",
+        out_shape=pltpu.VMEM((ROWS, 4 * PART + 128), F32),
+        in_specs=[VMEM] * 5,
+        out_specs=VMEM,
+        compiler_params=params(16),
+        cost_estimate=estimate,
+    )(carried[1], lhs, carried[5], low, share)
     pair = (kept + swapped(sent, "core").astype(F32)).astype(BF16)
     other = swapped(pair, "xh")
-    sent, kept = pl.pallas_call(
+    sent, scaled, squares = pl.pallas_call(
         third_kernel,
         name="third",
         out_shape=(
-            jax.ShapeDtypeStruct((34, ROWS, 128), BF16),
-            jax.ShapeDtypeStruct((34, ROWS, 128), F32),
+            pltpu.VMEM((34, ROWS, 128), BF16),
+            pltpu.VMEM((ROWS, PART), BF16),
+            pltpu.VMEM((ROWS, 128), F32),
         ),
         in_specs=[VMEM] * 4,
-        out_specs=(VMEM, VMEM),
+        out_specs=(VMEM,) * 3,
         compiler_params=params(16),
     )(pair, other, norm_gain, weight)
+    kept = pl.pallas_call(
+        last_kernel,
+        name="last",
+        out_shape=pltpu.VMEM((32, ROWS, 128), F32),
+        in_specs=[VMEM] * 2,
+        out_specs=VMEM,
+        compiler_params=params(16),
+        cost_estimate=estimate,
+    )(scaled, weight)
     arrived = swapped(sent, "core").astype(F32)
-    squares = kept[32] + kept[33] + arrived[32] + arrived[33]
-    scale = lax.rsqrt(squares * (1.0 / DV) + 1e-06)
-    part = ((kept[:32] + arrived[:32]) * scale).astype(BF16)
+    scale = lax.rsqrt((squares + arrived[32] + arrived[33]) * (1.0 / DV) + 1e-06)
+    part = ((kept + arrived[:32]) * scale).astype(BF16)
     landed = lax.all_to_all(part, ("xh", "head"), 0, 0, tiled=True)
     out = landed.astype(F32).sum(axis=0).astype(BF16)
     return out.reshape(SEQS, DRAFT, 128)

time: 47.9 us -> 46.6 us (0.973)
  waiting for transfers between devices: 5.81 us -> 4.68 us
    ppermute x3, waiting for transfers between devices: 5.81 us -> 4.68 us  [swapped(): return lax.ppermute(x, axis, [(0, 1), (1, 0)])]
    pallas_call x2 -> x4, Pallas kernels: 3.71 us -> 3.72 us  [the longest x1 2.08 us: body(): pl.pallas_call(second_kernel, name='second', out_shape=(pltpu.VMEM((ROWS,...]
  transfers between devices with their start and end apart: 3 -> 3, of which waited for: 3 -> 3; matrix products, arithmetic and copies ran while one was open for 0% -> 0% of each run, Pallas kernels for 0% -> 2%
where the time goes in v3:
time: 46.6 us; the launch traced here: 46.4 us
  blocking collectives  29.2 us (63%)
  Pallas kernels  7.78 us (17%)
  waiting for transfers between devices  4.68 us (10%)
  starting transfers between devices  3.24 us (7%)
  other arithmetic  0.84 us (2%)
  between operations  0.7 us (2%)
    all_to_all x1, blocking collectives, body(): landed = lax.all_to_all(part, ('xh', 'head'), 0, 0, tiled=True)  21.1 us
    all_gather x1, blocking collectives, body(): gathered = lax.all_gather(msg, KEY)  8.1 us
    ppermute x3, waiting for transfers between devices, swapped(): return lax.ppermute(x, axis, [(0, 1), (1, 0)])  4.68 us
    pallas_call x1, Pallas kernels, body(): pl.pallas_call(first_kernel, name='first', out_shape=(pltpu.VMEM((ROWS, D...  4.05 us
    ppermute x3, starting transfers between devices, swapped(): return lax.ppermute(x, axis, [(0, 1), (1, 0)])  3.24 us
    pallas_call x1, Pallas kernels, body(): pl.pallas_call(second_kernel, name='second', out_shape=(pltpu.VMEM((ROWS,...  2.08 us
  transfers between devices with their start and end apart: 3, of which 3 were waited for; matrix products, arithmetic and copies ran while one was open for 0% of the time, Pallas kernels for 2%

profile of v3, /device:TPU:0, one launch (start us, length us, event | category | flops | bytes accessed | tf_op | source)
XLA Modules:
  0.0 46.4 jit_solution(9130546859485910731)
XLA Ops:
  0.7 4.1 %first.1 = (bf16[32,1536]{1,0:T(8,128)(2,1)S(1)}, bf16[8,4,256,256]{3,2,1,0:T(8,128)(2,1)S(1)}, bf16[8,1024,256]{2,1,0:T(8,128)(2,1)S(1)}, f32[32,1024]{1,0:T(8,...) custom-call(bf16[8,4,1024]{2,1,0:T(4,128)(2,1)} %bitcast.37, ...), custom_call_target="tpu_custom_call" | custom-call | tf_op jit(solution)/shard_map/first/pallas_call | solution.py:287
  4.7 8.1 %all-gather = bf16[128,1536]{1,0:T(8,128)(2,1)S(1)} all-gather(bf16[32,1536]{1,0:T(8,128)(2,1)S(1)} %get-tuple-element.21), channel_id=2, replica_groups=mesh['xh'=2,'core'=2,'head'=16,'batch'=2] {'xh','core'}, dimensions={0}, use_global_device_ids=true | all-gather | bytes 491520 | tf_op jit(solution)/shard_map/all_gather | solution.py:315
  12.8 2.1 %second.1 = (bf16[32,1152]{1,0:T(8,128)(2,1)S(1)}, bf16[64,256]{1,0:T(8,128)(2,1)S(1)}, f32[32,512]{1,0:T(8,128)S(1)}, f32[32,128]{1,0:T(8,128)S(1)}) custom-call(f32[8,128]{1,0:T(8,128)S(1)} %broadcast_in_dim.10.ridge, bf16[4,32,1536]{2,1,0:T(8,128)(2,1)S(1)} %bitcast.34, bf16[8,4,256,256]{3,2,1,0:T(8,128)(2,1)S(1)} %get-tuple-element.22.cov, ...), custom_call_target="tpu_custom_call" | custom-call | tf_op jit(solution)/shard_map/second/pallas_call | solution.py:316
  14.9 0.0 copy-start
  14.9 0.0 copy-start.1
  14.9 0.4 collective-permute-start
  15.3 0.7 %own.1 = f32[32,1152]{1,0:T(8,128)S(1)} custom-call(bf16[8,1024,256]{2,1,0:T(8,128)(2,1)S(1)} %get-tuple-element.20.val, bf16[64,256]{1,0:T(8,128)(2,1)S(1)} %get-tuple-element.28.lhs, f32[32,128]{1,0:T(8,128)S(1)} %get-tuple-element.26.total_in, f32[32,512]{1,0:T(8,128)S(1)} %get-tuple-element.29.low, f32[32,128]{1,0:T(8,128)S(1)} %get-tuple-element.30.share), custom_call_target="tpu_custom_call" | custom-call | flops 268435456 | bytes 2097152 | tf_op jit(solution)/shard_map/own/pallas_call | solution.py:330
  16.0 0.3 collective-permute-done
  16.2 2.8 %collective-permute-start.1 = (bf16[32,1152]{1,0:T(8,128)(2,1)S(1)}, bf16[32,1152]{1,0:T(8,128)(2,1)S(1)}, u32[]{:S(2)}, u32[]{:S(2)}) collective-permute-start(bf16[32,1152]{1,0:T(8,128)(2,1)S(1)} %add_convert_fusion.mine), channel_id=1, source_target_pairs={{0,64},{64,0},{1,65},{65,1},{2,66},{66,2},{3,67},{67,3},{4,68},{68... | collective-permute-start | bytes 221192 | tf_op jit(solution)/shard_map/ppermute | solution.py:267
  19.0 3.3 %collective-permute-done.1.arrived = bf16[32,1152]{1,0:T(8,128)(2,1)S(1)} collective-permute-done((bf16[32,1152]{1,0:T(8,128)(2,1)S(1)}, bf16[32,1152]{1,0:T(8,128)(2,1)S(1)}, u32[]{:S(2)}, u32[]{:S(2)}) %collective-permute-start.1) | collective-permute-done | bytes 73760 | tf_op jit(solution)/shard_map/ppermute | solution.py:267
  22.4 0.0 copy-done
  22.4 0.0 copy-done.1
  22.4 0.5 %third.1 = (bf16[34,32,128]{2,1,0:T(8,128)(2,1)S(1)}, bf16[32,256]{1,0:T(8,128)(2,1)S(1)}, f32[32,128]{1,0:T(8,128)S(1)}) custom-call(bf16[32,1152]{1,0:T(8,128)(2,1)S(1)} %add_convert_fusion.mine, bf16[32,1152]{1,0:T(8,128)(2,1)S(1)} %collective-permute-done.1.arrived, f32[1,256]{1,0:T(1,128)S(1)} %copy-done.1, bf16[256,8192]{1,0:T(8,128)(2,1)S(1)} %bitcast.32), custom_call_target="tpu_custom_call" | custom-call | tf_op jit(solution)/shard_map/third/pallas_call | solution.py:341
  22.9 0.1 collective-permute-start.2
  23.0 0.5 %last.1 = f32[32,32,128]{2,1,0:T(8,128)S(1)} custom-call(bf16[32,256]{1,0:T(8,128)(2,1)S(1)} %get-tuple-element.32.scaled, bf16[256,8192]{1,0:T(8,128)(2,1)S(1)} %bitcast.33), custom_call_target="tpu_custom_call" | custom-call | flops 268435456 | bytes 2097152 | tf_op jit(solution)/shard_map/last/pallas_call | solution.py:353
  23.4 1.1 %collective-permute-done.2 = bf16[34,32,128]{2,1,0:T(8,128)(2,1)S(1)} collective-permute-done((bf16[34,32,128]{2,1,0:T(8,128)(2,1)S(1)}, bf16[34,32,128]{2,1,0:T(8,128)(2,1)S(1)}, u32[]{:S(2)}, u32[]{:S(2)}) %collective-permute-start.2) | collective-permute-done | bytes 278560 | tf_op jit(solution)/shard_map/ppermute | solution.py:267
  24.5 0.1 convert_element_type.16
  24.6 0.1 fusion.1
  24.7 21.1 %all_to_all.5 = bf16[32,32,128]{2,1,0:T(8,128)(2,1)S(1)} all-to-all(bf16[32,32,128]{2,1,0:T(8,128)(2,1)S(1)} %fusion.1), channel_id=1, replica_groups=mesh['xh'=2,'core'=2,'head'=16,'batch'=2] {'xh','head'}, dimensions={0} | all-to-all | bytes 524288 | tf_op jit(solution)/shard_map/all_to_all | solution.py:365
  45.8 0.6 %reduce_sum.12 = bf16[32,128]{1,0:T(8,128)(2,1)} reduce(bf16[32,32,128]{2,1,0:T(8,128)(2,1)S(1)} %all_to_all.5, bf16[]{:T(256)} %constant.6.clone.1), dimensions={0}, to_apply=%region_0.0 | reduce | flops 126976 | bytes 270338 | tf_op jit(solution)/shard_map/reduce_sum | solution.py:366
  (3 shorter events, 0.0 us)
Async XLA Ops:
  14.9 7.5 %copy-start = (bf16[1,256,8192]{2,1,0:T(8,128)(2,1)S(1)}, bf16[1,256,8192]{2,1,0:T(8,128)(2,1)}, u32[]{:S(2)}) copy-start(bf16[1,256,8192]{2,1,0:T(8,128)(2,1)} %param.19) | copy-start | bytes 12582916
  14.9 7.5 %copy-start.1 = (f32[1,256]{1,0:T(1,128)S(1)}, f32[1,256]{1,0:T(1,128)}, u32[]{:S(2)}) copy-start(f32[1,256]{1,0:T(1,128)} %gain.1) | copy-start | bytes 3076
  14.9 1.3 %collective-permute-start = (bf16[32,1152]{1,0:T(8,128)(2,1)S(1)}, bf16[32,1152]{1,0:T(8,128)(2,1)S(1)}, u32[]{:S(2)}, u32[]{:S(2)}) collective-permute-start(bf16[32,1152]{1,0:T(8,128)(2,1)S(1)} %get-tuple-element.31), channel_id=1, source_target_pairs={{0,32},{32,0},{1,33},{33,1},{2,34},{34,2},{3,35},{35,3},{4,36},{36... | collective-permute-start | bytes 221192 | tf_op jit(solution)/shard_map/ppermute | solution.py:267
  16.2 6.1 %collective-permute-start.1 = (bf16[32,1152]{1,0:T(8,128)(2,1)S(1)}, bf16[32,1152]{1,0:T(8,128)(2,1)S(1)}, u32[]{:S(2)}, u32[]{:S(2)}) collective-permute-start(bf16[32,1152]{1,0:T(8,128)(2,1)S(1)} %add_convert_fusion.mine), channel_id=1, source_target_pairs={{0,64},{64,0},{1,65},{65,1},{2,66},{66,2},{3,67},{67,3},{4,68},{68... | collective-permute-start | bytes 221192 | tf_op jit(solution)/shard_map/ppermute | solution.py:267
  22.9 1.6 %collective-permute-start.2 = (bf16[34,32,128]{2,1,0:T(8,128)(2,1)S(1)}, bf16[34,32,128]{2,1,0:T(8,128)(2,1)S(1)}, u32[]{:S(2)}, u32[]{:S(2)}) collective-permute-start(bf16[34,32,128]{2,1,0:T(8,128)(2,1)S(1)} %get-tuple-element.33), channel_id=1, source_target_pairs={{0,32},{32,0},{1,33},{33,1},{2,34},{34,2},{3,35},{35,3},{4,36},{36... | collective-permute-start | bytes 835592 | tf_op jit(solution)/shard_map/ppermute | solution.py:267

commit v4 on v3

--- a/solution.py
+++ b/solution.py
@@ -12,7 +12,8 @@
 DV = 1024
 PART = 256
 BLOCKS = DK // PART
-HEADS = 16
+SLOT = 2 * PART
+SHARE = 2 * SLOT
 F32 = jnp.float32
 BF16 = jnp.bfloat16
 KEY = ("xh", "core")
@@ -79,16 +80,19 @@
 
 def first_kernel(
     q_hbm, k_hbm, v_hbm, decay_hbm, write_hbm, cov_hbm, val_hbm,
-    msg, cov, val, q32, k32, v_mine, total_out, mix_out,
-    q_in, k_in, v_in, decay_in, write_in, z32, small_sem, big_sem, val_sem,
+    msg, cov, val, q32, k32, values, total_out, mix_out,
+    q_in, k_in, v_in, v_across, decay_in, write_in, small_sem, big_sem, val_sem,
 ):
-    start = pl.multiple_of(position()[0] * PART, PART)
+    me, core, xh = position()
+    start = pl.multiple_of(me * PART, PART)
+    across = pl.multiple_of((2 * (1 - xh) + core) * PART, PART)
     ends = [
         (decay_hbm, decay_in),
         (write_hbm, write_in),
         (q_hbm, q_in),
         (k_hbm, k_in),
         (v_hbm.at[:, :, pl.ds(start, PART)], v_in),
+        (v_hbm.at[:, :, pl.ds(across, PART)], v_across),
     ]
     small = [pltpu.make_async_copy(a, b, small_sem.at[n]) for n, (a, b) in enumerate(ends)]
     big = [
@@ -110,7 +114,8 @@
     total, mix = coefficients(decay_in[...], write_in[...])
     total_out[...] = jnp.broadcast_to(total, total_out.shape)
     mix_out[...] = mix
-    for c, x, out in zip(small[2:], (q_in, k_in, v_in), (q32, k32, v_mine)):
+    out_of = (q32, k32, values.at[:, :PART], values.at[:, PART:])
+    for c, x, out in zip(small[2:], (q_in, k_in, v_in, v_across), out_of):
         c.wait()
         stack(x, out)
     keys = k32[...].astype(BF16)
@@ -123,7 +128,7 @@
         both = jnp.concatenate(pieces, axis=0)
         res = [jnp.concatenate([mm(both, cov[2 * p + n, b]) for b in range(BLOCKS)], axis=1) for n in range(2)]
         z = jnp.where(first, res[0][:8] + res[0][8:], res[1][:8] + res[1][8:])
-        z32[8 * p : 8 * p + 8, :] = z * total[8 * p : 8 * p + 8]
+        msg[8 * p : 8 * p + 8, :DK] = (z * total[8 * p : 8 * p + 8]).astype(BF16)
 
     held = None
     for p in range(SEQS // 2):
@@ -141,45 +146,48 @@
         if held is not None:
             by_columns(*held)
         held = (p, pieces)
-    y_hi, y_lo = msg[:, DK : DK + PART], msg[:, DK + PART :]
-    dots = mm(y_hi, keys_mine, NT) + mm(y_lo, keys_mine, NT)
-    low_rank = mm_wide(mix * dots, keys)
     by_columns(*held)
-    msg[:, :DK] = (z32[...] + low_rank).astype(BF16)
     big[4][0].wait()
 
 
 def second_kernel(
-    ridge, gathered, cov, val, q32, k32, v_mine, total_in, mix_in, sent, lhs, low, share_out,
-    y32, w32, d32, x32, aw32,
+    ridge, gathered, cov, val, q32, k32, values_in, total_in, mix_in, sent, lhs, low, share_out,
+    p32, y32, w32, low32, d32, x32, ap32, aw32, dm32,
 ):
     total, shift, mix = total_in[:, :1], ridge[0:1, 0:1], mix_in[...]
-    me, core, _ = position()
+    me, core, xh = position()
     mine = pl.ds(pl.multiple_of(me * PART, PART), PART)
     first = lax.broadcasted_iota(jnp.int32, (8, 1), 0) < DRAFT
 
     def dot(a, b):
         return jnp.sum(a * b, axis=1, keepdims=True)
 
-    for g in range(4):
-        y32[:, g * PART : (g + 1) * PART] = gathered[g, :, DK : DK + PART].astype(F32) + gathered[
+    def dots_of(a, b):
+        res = mm(jnp.concatenate(halves(a), axis=0), b, NT)
+        return res[:ROWS] + res[ROWS:]
+
+    for g in range(BLOCKS):
+        p32[:, g * PART : (g + 1) * PART] = gathered[g, :, DK : DK + PART].astype(F32) + gathered[
             g, :, DK + PART :
         ].astype(F32)
-    w = y32[...]
-    y32[...] = w + shift * q32[...]
-    w = shift * (w + y32[...])
-    for g in range(4):
-        w = w + gathered[g, :, :DK].astype(F32)
-    w32[...] = w
     keys = k32[...].astype(BF16)
     keys_mine = k32[:, mine].astype(BF16)
+    low32[...] = mm_wide(mix * dots_of(p32[...], keys), keys)
+    p = p32[...]
+    y = p + shift * q32[...]
+    y32[...] = y
+    w = shift * (p + y)
+    for g in range(BLOCKS):
+        w = w + gathered[g, :, :DK].astype(F32)
+    w32[...] = w + low32[...]
     for p in range(SEQS // 2):
         rows = slice(8 * p, 8 * p + 8)
-        pieces = jnp.concatenate(halves(w32[rows, :]), axis=0)
+        pieces = jnp.concatenate(halves(p32[rows, :]) + halves(w32[rows, :]), axis=0)
         res = [by_rows(pieces, cov, 2 * p + n) for n in range(2)]
-        aw32[rows, :] = jnp.where(first, res[0][:8] + res[0][8:], res[1][:8] + res[1][8:]) * total[rows]
-    dots_w = mm(jnp.concatenate(halves(w32[...]), axis=0), keys, NT)
-    image_w = aw32[...] + mm_wide(mix * (dots_w[:ROWS] + dots_w[ROWS:]), keys_mine) + shift * w32[:, mine]
+        res = [(r[:8] + r[8:16], r[16:24] + r[24:]) for r in res]
+        ap32[rows, :] = jnp.where(first, res[0][0], res[1][0]) * total[rows]
+        aw32[rows, :] = jnp.where(first, res[0][1], res[1][1]) * total[rows]
+    image_w = aw32[...] + mm_wide(mix * dots_of(w32[...], keys), keys_mine) + shift * w32[:, mine]
 
     q, y, w = q32[...], y32[...], w32[...]
     rr0 = dot(q, q)
@@ -194,47 +202,55 @@
     res2 = res1 - a1 * image1
     rr2 = dot(res2, res2)
     b1 = rr2 / rr1
-    dir2 = res2 + b1 * dir1
-    d32[...] = dir2
+    d32[...] = res2 + b1 * dir1
     x32[...] = sol2
-    y, w = y32[:, mine], w32[:, mine]
-    image2 = y - a0 * w - a1 * ((1.0 + b0) * w - a0 * image_w) + b1 * ((1.0 + b0) * y - a0 * w)
-    share = jnp.broadcast_to(dot(d32[:, mine], image2) / rr2, (ROWS, 128))
-    sent[:, 4 * PART :] = share.astype(BF16)
+    q, y, p = q32[:, mine], y32[:, mine], p32[:, mine]
+    w = ap32[...] + low32[:, mine] + shift * (p + y)
+    res1 = q - a0 * y
+    dir1 = res1 + b0 * q
+    image1 = (1.0 + b0) * y - a0 * w
+    dir2 = res1 - a1 * image1 + b1 * dir1
+    dm32[...] = dir2
+    image2 = y - a0 * w - a1 * ((1.0 + b0) * w - a0 * image_w) + b1 * image1
+    known = d32[:, mine]
+    share = jnp.broadcast_to(dot(known, image2) / rr2, (ROWS, 64))
+    missed = mix * mm((dir2 - known).astype(BF16), keys_mine, NT)
+    share = jnp.concatenate([share, missed, jnp.zeros((ROWS, 32), F32)], axis=1)
     share_out[...] = share
     for p in range(SEQS // 2):
         rows = slice(8 * p, 8 * p + 8)
-        both = [x32[rows, mine].astype(BF16), d32[rows, mine].astype(BF16)]
+        both = [x32[rows, mine].astype(BF16), dm32[rows, :].astype(BF16)]
         lhs[2 * 8 * p : 2 * 8 * (p + 1), :] = jnp.concatenate(both, axis=0)
         if p == 2:
             dots = mm(jnp.concatenate(halves(x32[...]) + (d32[...].astype(BF16),), axis=0), keys, NT)
-        by_values(lhs, val, total, 1 - core, p, sent)
-    values = v_mine[...].astype(BF16)
+        by_values(lhs, val, total, xh, 1 - core, p, sent)
+    sent[:, SHARE:] = share.astype(BF16)
+    values = values_in[:, :PART].astype(BF16)
     low[:, :PART] = mm_wide(mix * (dots[:ROWS] + dots[ROWS : 2 * ROWS]), values)
     low[:, PART:] = mm_wide(mix * dots[2 * ROWS :], values)
 
 
-def by_values(lhs, val, total, core, p, out):
+def by_values(lhs, val, total, xh, core, p, out):
     rows = slice(8 * p, 8 * p + 8)
     first = lax.broadcasted_iota(jnp.int32, (8, 1), 0) < DRAFT
     both = lhs[16 * p : 16 * p + 16, :]
-    for x in range(2):
+    for slot, x in enumerate((xh, 1 - xh)):
         entries = pl.ds(pl.multiple_of((2 * x + core) * PART, PART), PART)
         res = [mm(both, val[2 * p + n, entries, :], NT) for n in range(2)]
         for m in range(2):
             half = slice(8 * m, 8 * m + 8)
             part = jnp.where(first, res[0][half], res[1][half]) * total[rows]
-            out[rows, (2 * m + x) * PART : (2 * m + x + 1) * PART] = part.astype(out.dtype)
+            at = slot * SLOT + m * PART
+            out[rows, at : at + PART] = part.astype(out.dtype)
 
 
 def own_kernel(val, lhs, total_in, low, share, kept):
     _, core, xh = position()
     total = total_in[:, :1]
     for p in range(SEQS // 2):
-        by_values(lhs, val, total, core, p, kept)
-    kept[:, 4 * PART :] = share[...]
-    for m in range(2):
-        kept[:, pl.ds(pl.multiple_of((2 * m + xh) * PART, PART), PART)] += low[:, m * PART : (m + 1) * PART]
+        by_values(lhs, val, total, xh, core, p, kept)
+    kept[:, SHARE:] = share[...]
+    kept[:, : 2 * PART] += low[...]
 
 
 def project(scaled, weight, core, out):
@@ -247,20 +263,32 @@
                 out[16 * x + n * (step // 128) + m] = part[:, 128 * m : 128 * (m + 1)].astype(out.dtype)
 
 
-def third_kernel(mine, arrived, gain, weight, sent, scaled, squares):
-    _, core, xh = position()
-    total = mine[...].astype(F32) + arrived[...].astype(F32)
-    a2 = 1.0 / total[:, 4 * PART : 4 * PART + 1]
-    readout = total[:, : 2 * PART] + a2 * total[:, 2 * PART : 4 * PART]
-    own = jnp.where(xh == 0, readout[:, :PART], readout[:, PART:])
-    scaled[...] = (own * gain[...]).astype(BF16)
-    project(scaled[...], weight, 1 - core, sent)
-    squares[...] = jnp.broadcast_to(jnp.sum(readout * readout, axis=1, keepdims=True), (ROWS, 128))
+def third_kernel(mine, partner, arrived, values, gain, weight, sent, scaled, squares):
+    pair = mine[...] + partner[...].astype(F32)
+    other = arrived[...].astype(F32)
+    total = [pair[:, SLOT * n : SLOT * (n + 1)] + other[:, SLOT * (1 - n) : SLOT * (2 - n)] for n in range(2)]
+    share = pair[:, SHARE:] + other[:, SHARE:]
+    a2 = 1.0 / share[:, :1]
+    missed = mm(share[:, 64:96].astype(BF16), values[...].astype(BF16))
+    readout = [
+        total[n][:, :PART] + a2 * (total[n][:, PART:] + missed[:, PART * n : PART * (n + 1)]) for n in range(2)
+    ]
+    scaled[...] = (readout[0] * gain[...]).astype(BF16)
+    project(scaled[...], weight, 1 - position()[1], sent)
+    both = readout[0] * readout[0] + readout[1] * readout[1]
+    squares[...] = jnp.broadcast_to(jnp.sum(both, axis=1, keepdims=True), (ROWS, 128))
     sent[32], sent[33] = halves(squares[...])
 
 
 def last_kernel(scaled, weight, kept):
     project(scaled[...], weight, position()[1], kept)
+
+
+def join_kernel(kept, arrived, squares, out):
+    sums = squares[...] + arrived[32].astype(F32) + arrived[33].astype(F32)
+    scale = lax.rsqrt(sums * (1.0 / DV) + 1e-06)
+    for n in range(32):
+        out[n] = ((kept[n] + arrived[n].astype(F32)) * scale).astype(BF16)
 
 
 def swapped(x, axis):
@@ -293,7 +321,7 @@
             pltpu.VMEM((SEQS, DV, PART), BF16),
             pltpu.VMEM((ROWS, DK), F32),
             pltpu.VMEM((ROWS, DK), F32),
-            pltpu.VMEM((ROWS, PART), F32),
+            pltpu.VMEM((ROWS, SLOT), F32),
             pltpu.VMEM((ROWS, 128), F32),
             pltpu.VMEM((ROWS, ROWS), F32),
         ),
@@ -303,10 +331,10 @@
             pltpu.VMEM((SEQS, DRAFT, DK), BF16),
             pltpu.VMEM((SEQS, DRAFT, DK), BF16),
             pltpu.VMEM((SEQS, DRAFT, PART), BF16),
+            pltpu.VMEM((SEQS, DRAFT, PART), BF16),
             pltpu.VMEM((DRAFT, SEQS), F32),
             pltpu.VMEM((DRAFT, SEQS), F32),
-            pltpu.VMEM((ROWS, DK), F32),
-            pltpu.SemaphoreType.DMA((5,)),
+            pltpu.SemaphoreType.DMA((6,)),
             pltpu.SemaphoreType.DMA((SEQS // 2, BLOCKS)),
             pltpu.SemaphoreType.DMA,
         ],
@@ -317,27 +345,27 @@
         second_kernel,
         name="second",
         out_shape=(
-            pltpu.VMEM((ROWS, 4 * PART + 128), BF16),
+            pltpu.VMEM((ROWS, SHARE + 128), BF16),
             pltpu.VMEM((2 * ROWS, PART), BF16),
             pltpu.VMEM((ROWS, 2 * PART), F32),
             pltpu.VMEM((ROWS, 128), F32),
         ),
         in_specs=[VMEM] * 9,
         out_specs=(VMEM,) * 4,
-        scratch_shapes=[pltpu.VMEM((ROWS, n), F32) for n in (DK, DK, DK, DK, PART)],
+        scratch_shapes=[pltpu.VMEM((ROWS, n), F32) for n in [DK] * 6 + [PART] * 3],
         compiler_params=params(16),
     )(jnp.broadcast_to(ridge_shift[None], (8, 128)), gathered, *carried)
     kept = pl.pallas_call(
         own_kernel,
         name="own",
-        out_shape=pltpu.VMEM((ROWS, 4 * PART + 128), F32),
+        out_shape=pltpu.VMEM((ROWS, SHARE + 128), F32),
         in_specs=[VMEM] * 5,
         out_specs=VMEM,
         compiler_params=params(16),
         cost_estimate=estimate,
     )(carried[1], lhs, carried[5], low, share)
-    pair = (kept + swapped(sent, "core").astype(F32)).astype(BF16)
-    other = swapped(pair, "xh")
+    partner = swapped(sent, "core")
+    other = swapped((kept + partner.astype(F32)).astype(BF16), "xh")
     sent, scaled, squares = pl.pallas_call(
         third_kernel,
         name="third",
@@ -346,11 +374,11 @@
             pltpu.VMEM((ROWS, PART), BF16),
             pltpu.VMEM((ROWS, 128), F32),
         ),
-        in_specs=[VMEM] * 4,
+        in_specs=[VMEM] * 6,
         out_specs=(VMEM,) * 3,
         compiler_params=params(16),
-    )(pair, other, norm_gain, weight)
-    kept = pl.pallas_call(
+    )(kept, partner, other, carried[4], norm_gain, weight)
+    part = pl.pallas_call(
         last_kernel,
         name="last",
         out_shape=pltpu.VMEM((32, ROWS, 128), F32),
@@ -359,12 +387,16 @@
         compiler_params=params(16),
         cost_estimate=estimate,
     )(scaled, weight)
-    arrived = swapped(sent, "core").astype(F32)
-    scale = lax.rsqrt((squares + arrived[32] + arrived[33]) * (1.0 / DV) + 1e-06)
-    part = ((kept + arrived[:32]) * scale).astype(BF16)
+    part = pl.pallas_call(
+        join_kernel,
+        name="join",
+        out_shape=pltpu.VMEM((32, ROWS, 128), BF16),
+        in_specs=[VMEM] * 3,
+        out_specs=VMEM,
+        compiler_params=params(16),
+    )(part, swapped(sent, "core"), squares)
     landed = lax.all_to_all(part, ("xh", "head"), 0, 0, tiled=True)
-    out = landed.astype(F32).sum(axis=0).astype(BF16)
-    return out.reshape(SEQS, DRAFT, 128)
+    return landed.astype(F32).sum(axis=0).astype(BF16).reshape(SEQS, DRAFT, 128)
 
 
 def solution(mesh):

time: 46.6 us -> 46.9 us (level)
  no operation moved by 1% of the time
where the time goes in v4:
time: 46.9 us; the launch traced here: 46.7 us
  blocking collectives  29.2 us (62%)
  Pallas kernels  8.19 us (17%)
  waiting for transfers between devices  4.69 us (10%)
  starting transfers between devices  3.23 us (7%)
  between operations  0.68 us (1%)
  other arithmetic  0.66 us (1%)
    all_to_all x1, blocking collectives, body(): landed = lax.all_to_all(part, ('xh', 'head'), 0, 0, tiled=True)  21.1 us
    all_gather x1, blocking collectives, body(): gathered = lax.all_gather(msg, KEY)  8.1 us
    ppermute x3, waiting for transfers between devices, swapped(): return lax.ppermute(x, axis, [(0, 1), (1, 0)])  4.69 us
    pallas_call x1, Pallas kernels, body(): pl.pallas_call(first_kernel, name='first', out_shape=(pltpu.VMEM((ROWS, D...  4.08 us
    ppermute x3, starting transfers between devices, swapped(): return lax.ppermute(x, axis, [(0, 1), (1, 0)])  3.23 us
    pallas_call x1, Pallas kernels, body(): pl.pallas_call(second_kernel, name='second', out_shape=(pltpu.VMEM((ROWS,...  2.3 us
  transfers between devices with their start and end apart: 3, of which 3 were waited for; matrix products, arithmetic and copies ran while one was open for 0% of the time, Pallas kernels for 2%

profile of v4, /device:TPU:0, one launch (start us, length us, event | category | flops | bytes accessed | tf_op | source)
XLA Modules:
  0.0 46.7 jit_solution(14937633714484745361)
XLA Ops:
  0.7 4.1 %first.1 = (bf16[32,1536]{1,0:T(8,128)(2,1)S(1)}, bf16[8,4,256,256]{3,2,1,0:T(8,128)(2,1)S(1)}, bf16[8,1024,256]{2,1,0:T(8,128)(2,1)S(1)}, f32[32,1024]{1,0:T(8,...) custom-call(bf16[8,4,1024]{2,1,0:T(4,128)(2,1)} %bitcast.21, ...), custom_call_target="tpu_custom_call" | custom-call | tf_op jit(solution)/shard_map/first/pallas_call | solution.py:315
  4.7 8.1 %all-gather = bf16[128,1536]{1,0:T(8,128)(2,1)S(1)} all-gather(bf16[32,1536]{1,0:T(8,128)(2,1)S(1)} %get-tuple-element.21), channel_id=2, replica_groups=mesh['xh'=2,'core'=2,'head'=16,'batch'=2] {'xh','core'}, dimensions={0}, use_global_device_ids=true | all-gather | bytes 491520 | tf_op jit(solution)/shard_map/all_gather | solution.py:343
  12.8 2.3 %second.1 = (bf16[32,1152]{1,0:T(8,128)(2,1)S(1)}, bf16[64,256]{1,0:T(8,128)(2,1)S(1)}, f32[32,512]{1,0:T(8,128)S(1)}, f32[32,128]{1,0:T(8,128)S(1)}) custom-call(f32[8,128]{1,0:T(8,128)S(1)} %broadcast_in_dim.9.ridge, bf16[4,32,1536]{2,1,0:T(8,128)(2,1)S(1)} %bitcast.18, bf16[8,4,256,256]{3,2,1,0:T(8,128)(2,1)S(1)} %get-tuple-element.22.cov, ...), custom_call_target="tpu_custom_call" | custom-call | tf_op jit(solution)/shard_map/second/pallas_call | solution.py:344
  15.1 0.0 copy-start
  15.1 0.0 copy-start.1
  15.1 0.4 collective-permute-start
  15.6 0.6 %own.1.mine = f32[32,1152]{1,0:T(8,128)S(1)} custom-call(bf16[8,1024,256]{2,1,0:T(8,128)(2,1)S(1)} %get-tuple-element.20.val, bf16[64,256]{1,0:T(8,128)(2,1)S(1)} %get-tuple-element.28.lhs, f32[32,128]{1,0:T(8,128)S(1)} %get-tuple-element.26.total_in, f32[32,512]{1,0:T(8,128)S(1)} %get-tuple-element.29.low, f32[32,128]{1,0:T(8,128)S(1)} %get-tuple-element.30.share), custom_call_target="tpu_custom_call" | custom-call | flops 268435456 | bytes 2097152 | tf_op jit(solution)/shard_map/own/pallas_call | solution.py:358
  16.2 0.3 collective-permute-done.partner
  16.5 2.8 %collective-permute-start.1 = (bf16[32,1152]{1,0:T(8,128)(2,1)S(1)}, bf16[32,1152]{1,0:T(8,128)(2,1)S(1)}, u32[]{:S(2)}, u32[]{:S(2)}) collective-permute-start(bf16[32,1152]{1,0:T(8,128)(2,1)S(1)} %add_convert_fusion), channel_id=1, source_target_pairs={{0,64},{64,0},{1,65},{65,1},{2,66},{66,2},{3,67},{67,3},{4,68},{68... | collective-permute-start | bytes 221192 | tf_op jit(solution)/shard_map/ppermute | solution.py:295
  19.2 3.3 %collective-permute-done.1.arrived = bf16[32,1152]{1,0:T(8,128)(2,1)S(1)} collective-permute-done((bf16[32,1152]{1,0:T(8,128)(2,1)S(1)}, bf16[32,1152]{1,0:T(8,128)(2,1)S(1)}, u32[]{:S(2)}, u32[]{:S(2)}) %collective-permute-start.1) | collective-permute-done | bytes 73760 | tf_op jit(solution)/shard_map/ppermute | solution.py:295
  22.6 0.0 copy-done
  22.6 0.0 copy-done.1
  22.6 0.6 %third.1 = (bf16[34,32,128]{2,1,0:T(8,128)(2,1)S(1)}, bf16[32,256]{1,0:T(8,128)(2,1)S(1)}, f32[32,128]{1,0:T(8,128)S(1)}) custom-call(f32[32,1152]{1,0:T(8,128)S(1)} %own.1.mine, bf16[32,1152]{1,0:T(8,128)(2,1)S(1)} %collective-permute-done.partner, bf16[32,1152]{1,0:T(8,128)(2,1)S(1)} %collective-permute-done.1.arrived, ...), custom_call_target="tpu_custom_call" | custom-call | tf_op jit(solution)/shard_map/third/pallas_call | solution.py:369
  23.2 0.1 collective-permute-start.2
  23.3 0.5 %last.1.kept = f32[32,32,128]{2,1,0:T(8,128)S(1)} custom-call(bf16[32,256]{1,0:T(8,128)(2,1)S(1)} %get-tuple-element.32.scaled, bf16[256,8192]{1,0:T(8,128)(2,1)S(1)} %bitcast.17), custom_call_target="tpu_custom_call" | custom-call | flops 268435456 | bytes 2097152 | tf_op jit(solution)/shard_map/last/pallas_call | solution.py:381
  23.8 1.1 %collective-permute-done.2.arrived = bf16[34,32,128]{2,1,0:T(8,128)(2,1)S(1)} collective-permute-done((bf16[34,32,128]{2,1,0:T(8,128)(2,1)S(1)}, bf16[34,32,128]{2,1,0:T(8,128)(2,1)S(1)}, u32[]{:S(2)}, u32[]{:S(2)}) %collective-permute-start.2) | collective-permute-done | bytes 278560 | tf_op jit(solution)/shard_map/ppermute | solution.py:295
  24.9 0.1 join.1
  24.9 21.1 %all_to_all.5 = bf16[32,32,128]{2,1,0:T(8,128)(2,1)S(1)} all-to-all(bf16[32,32,128]{2,1,0:T(8,128)(2,1)S(1)} %join.1), channel_id=1, replica_groups=mesh['xh'=2,'core'=2,'head'=16,'batch'=2] {'xh','head'}, dimensions={0} | all-to-all | bytes 524288 | tf_op jit(solution)/shard_map/all_to_all | solution.py:398
  46.0 0.6 %reduce_sum.12 = bf16[32,128]{1,0:T(8,128)(2,1)} reduce(bf16[32,32,128]{2,1,0:T(8,128)(2,1)S(1)} %all_to_all.5, bf16[]{:T(256)} %constant.2.clone.1), dimensions={0}, to_apply=%region_0.0 | reduce | flops 126976 | bytes 270338 | tf_op jit(solution)/shard_map/reduce_sum | solution.py:399
  (2 shorter events, 0.0 us)
Async XLA Ops:
  15.1 7.5 %copy-start = (bf16[1,256,8192]{2,1,0:T(8,128)(2,1)S(1)}, bf16[1,256,8192]{2,1,0:T(8,128)(2,1)}, u32[]{:S(2)}) copy-start(bf16[1,256,8192]{2,1,0:T(8,128)(2,1)} %param.19) | copy-start | bytes 12582916
  15.1 7.5 %copy-start.1 = (f32[1,256]{1,0:T(1,128)S(1)}, f32[1,256]{1,0:T(1,128)}, u32[]{:S(2)}) copy-start(f32[1,256]{1,0:T(1,128)} %gain.1) | copy-start | bytes 3076
  15.1 1.3 %collective-permute-start = (bf16[32,1152]{1,0:T(8,128)(2,1)S(1)}, bf16[32,1152]{1,0:T(8,128)(2,1)S(1)}, u32[]{:S(2)}, u32[]{:S(2)}) collective-permute-start(bf16[32,1152]{1,0:T(8,128)(2,1)S(1)} %get-tuple-element.31), channel_id=1, source_target_pairs={{0,32},{32,0},{1,33},{33,1},{2,34},{34,2},{3,35},{35,3},{4,36},{36... | collective-permute-start | bytes 221192 | tf_op jit(solution)/shard_map/ppermute | solution.py:295
  16.5 6.1 %collective-permute-start.1 = (bf16[32,1152]{1,0:T(8,128)(2,1)S(1)}, bf16[32,1152]{1,0:T(8,128)(2,1)S(1)}, u32[]{:S(2)}, u32[]{:S(2)}) collective-permute-start(bf16[32,1152]{1,0:T(8,128)(2,1)S(1)} %add_convert_fusion), channel_id=1, source_target_pairs={{0,64},{64,0},{1,65},{65,1},{2,66},{66,2},{3,67},{67,3},{4,68},{68... | collective-permute-start | bytes 221192 | tf_op jit(solution)/shard_map/ppermute | solution.py:295
  23.2 1.6 %collective-permute-start.2 = (bf16[34,32,128]{2,1,0:T(8,128)(2,1)S(1)}, bf16[34,32,128]{2,1,0:T(8,128)(2,1)S(1)}, u32[]{:S(2)}, u32[]{:S(2)}) collective-permute-start(bf16[34,32,128]{2,1,0:T(8,128)(2,1)S(1)} %get-tuple-element.33), channel_id=1, source_target_pairs={{0,32},{32,0},{1,33},{33,1},{2,34},{34,2},{3,35},{35,3},{4,36},{36... | collective-permute-start | bytes 835592 | tf_op jit(solution)/shard_map/ppermute | solution.py:295

commit v5 on v4

--- a/solution.py
+++ b/solution.py
@@ -80,7 +80,7 @@
 
 def first_kernel(
     q_hbm, k_hbm, v_hbm, decay_hbm, write_hbm, cov_hbm, val_hbm,
-    msg, cov, val, q32, k32, values, total_out, mix_out,
+    msg, cov, val, q32, k32, values, total_out, mix_out, ck, cq,
     q_in, k_in, v_in, v_across, decay_in, write_in, small_sem, big_sem, val_sem,
 ):
     me, core, xh = position()
@@ -107,7 +107,7 @@
         for p in range(SEQS // 2)
     ]
     big.append([pltpu.make_async_copy(val_hbm, val, val_sem)])
-    for c in small + big[0] + big[1] + big[2] + big[3]:
+    for c in small[:4] + big[0] + small[4:] + big[1] + big[2] + big[3] + big[4]:
         c.start()
     for c in small[:2]:
         c.wait()
@@ -134,12 +134,13 @@
     for p in range(SEQS // 2):
         for c in big[p]:
             c.wait()
-        if p == 0:
-            for c in big[4]:
-                c.start()
-        slab = q32[8 * p : 8 * p + 8, :].astype(BF16)
+        rows = slice(8 * p, 8 * p + 8)
+        slab = jnp.concatenate([q32[rows, :].astype(BF16), k32[rows, :].astype(BF16)], axis=0)
         res = [by_rows(slab, cov, 2 * p + n) for n in range(2)]
-        y = jnp.where(first, res[0], res[1]) * total[8 * p : 8 * p + 8] + base[8 * p : 8 * p + 8]
+        ck[rows, :] = jnp.where(first, res[0][8:], res[1][8:])
+        part = jnp.where(first, res[0][:8], res[1][:8]) * total[rows]
+        cq[rows, :] = part
+        y = part + base[rows]
         pieces = halves(y)
         msg[8 * p : 8 * p + 8, DK : DK + PART] = pieces[0]
         msg[8 * p : 8 * p + 8, DK + PART :] = pieces[1]
@@ -151,8 +152,8 @@
 
 
 def second_kernel(
-    ridge, gathered, cov, val, q32, k32, values_in, total_in, mix_in, sent, lhs, low, share_out,
-    p32, y32, w32, low32, d32, x32, ap32, aw32, dm32,
+    ridge, gathered, cov, val, q32, k32, values_in, total_in, mix_in, ck, cq, sent, lhs, low, share_out,
+    p32, c32, y32, w32, low32, d32, x32, ap32, ac32, dm32,
 ):
     total, shift, mix = total_in[:, :1], ridge[0:1, 0:1], mix_in[...]
     me, core, xh = position()
@@ -172,22 +173,26 @@
         ].astype(F32)
     keys = k32[...].astype(BF16)
     keys_mine = k32[:, mine].astype(BF16)
-    low32[...] = mm_wide(mix * dots_of(p32[...], keys), keys)
-    p = p32[...]
-    y = p + shift * q32[...]
-    y32[...] = y
-    w = shift * (p + y)
-    for g in range(BLOCKS):
-        w = w + gathered[g, :, :DK].astype(F32)
-    w32[...] = w + low32[...]
+    c = gathered[0, :, :DK].astype(F32)
+    for g in range(1, BLOCKS):
+        c = c + gathered[g, :, :DK].astype(F32)
+    c32[...] = c
+    coef = mix * dots_of(p32[...], keys)
     for p in range(SEQS // 2):
         rows = slice(8 * p, 8 * p + 8)
-        pieces = jnp.concatenate(halves(p32[rows, :]) + halves(w32[rows, :]), axis=0)
+        pieces = jnp.concatenate(halves(p32[rows, :]) + halves(c32[rows, :]), axis=0)
         res = [by_rows(pieces, cov, 2 * p + n) for n in range(2)]
         res = [(r[:8] + r[8:16], r[16:24] + r[24:]) for r in res]
         ap32[rows, :] = jnp.where(first, res[0][0], res[1][0]) * total[rows]
-        aw32[rows, :] = jnp.where(first, res[0][1], res[1][1]) * total[rows]
-    image_w = aw32[...] + mm_wide(mix * dots_of(w32[...], keys), keys_mine) + shift * w32[:, mine]
+        ac32[rows, :] = jnp.where(first, res[0][1], res[1][1]) * total[rows]
+        if p == 0:
+            low32[...] = mm_wide(coef, keys)
+            y32[...] = p32[...] + shift * q32[...]
+            w32[...] = c32[...] + low32[...] + shift * (p32[...] + y32[...])
+    ck_hi, ck_lo = halves(ck[...])
+    state_w = ac32[...] + total * (mm_wide(coef, ck_hi) + mm(coef.astype(BF16), ck_lo))
+    state_w = state_w + shift * (2.0 * ap32[...] + shift * cq[...])
+    image_w = state_w + mm_wide(mix * dots_of(w32[...], keys), keys_mine) + shift * w32[:, mine]
 
     q, y, w = q32[...], y32[...], w32[...]
     rr0 = dot(q, q)
@@ -324,9 +329,11 @@
             pltpu.VMEM((ROWS, SLOT), F32),
             pltpu.VMEM((ROWS, 128), F32),
             pltpu.VMEM((ROWS, ROWS), F32),
+            pltpu.VMEM((ROWS, PART), F32),
+            pltpu.VMEM((ROWS, PART), F32),
         ),
         in_specs=[HBM] * 7,
-        out_specs=(VMEM,) * 8,
+        out_specs=(VMEM,) * 10,
         scratch_shapes=[
             pltpu.VMEM((SEQS, DRAFT, DK), BF16),
             pltpu.VMEM((SEQS, DRAFT, DK), BF16),
@@ -350,9 +357,9 @@
             pltpu.VMEM((ROWS, 2 * PART), F32),
             pltpu.VMEM((ROWS, 128), F32),
         ),
-        in_specs=[VMEM] * 9,
+        in_specs=[VMEM] * 11,
         out_specs=(VMEM,) * 4,
-        scratch_shapes=[pltpu.VMEM((ROWS, n), F32) for n in [DK] * 6 + [PART] * 3],
+        scratch_shapes=[pltpu.VMEM((ROWS, n), F32) for n in [DK] * 7 + [PART] * 3],
         compiler_params=params(16),
     )(jnp.broadcast_to(ridge_shift[None], (8, 128)), gathered, *carried)
     kept = pl.pallas_call(

time: 46.9 us -> 46.6 us (level)
  no operation moved by 1% of the time
where the time goes in v5:
time: 46.6 us; the launch traced here: 46.4 us
  blocking collectives  29.2 us (63%)
  Pallas kernels  7.91 us (17%)
  waiting for transfers between devices  4.69 us (10%)
  starting transfers between devices  3.24 us (7%)
  between operations  0.68 us (1%)
  other arithmetic  0.66 us (1%)
    all_to_all x1, blocking collectives, body(): landed = lax.all_to_all(part, ('xh', 'head'), 0, 0, tiled=True)  21.1 us
    all_gather x1, blocking collectives, body(): gathered = lax.all_gather(msg, KEY)  8.1 us
    ppermute x3, waiting for transfers between devices, swapped(): return lax.ppermute(x, axis, [(0, 1), (1, 0)])  4.69 us
    pallas_call x1, Pallas kernels, body(): pl.pallas_call(first_kernel, name='first', out_shape=(pltpu.VMEM((ROWS, D...  3.88 us
    ppermute x3, starting transfers between devices, swapped(): return lax.ppermute(x, axis, [(0, 1), (1, 0)])  3.24 us
    pallas_call x1, Pallas kernels, body(): pl.pallas_call(second_kernel, name='second', out_shape=(pltpu.VMEM((ROWS,...  2.21 us
  transfers between devices with their start and end apart: 3, of which 3 were waited for; matrix products, arithmetic and copies ran while one was open for 0% of the time, Pallas kernels for 2%

profile of v5, /device:TPU:0, one launch (start us, length us, event | category | flops | bytes accessed | tf_op | source)
XLA Modules:
  0.0 46.4 jit_solution(8292892366393375967)
XLA Ops:
  0.7 3.9 %first.1 = (bf16[32,1536]{1,0:T(8,128)(2,1)S(1)}, bf16[8,4,256,256]{3,2,1,0:T(8,128)(2,1)S(1)}, bf16[8,1024,256]{2,1,0:T(8,128)(2,1)S(1)}, f32[32,1024]{1,0:T(8,...) custom-call(bf16[8,4,1024]{2,1,0:T(4,128)(2,1)} %bitcast.21, ...), custom_call_target="tpu_custom_call" | custom-call | tf_op jit(solution)/shard_map/first/pallas_call | solution.py:320
  4.5 8.1 %all-gather = bf16[128,1536]{1,0:T(8,128)(2,1)S(1)} all-gather(bf16[32,1536]{1,0:T(8,128)(2,1)S(1)} %get-tuple-element.23), channel_id=2, replica_groups=mesh['xh'=2,'core'=2,'head'=16,'batch'=2] {'xh','core'}, dimensions={0}, use_global_device_ids=true | all-gather | bytes 491520 | tf_op jit(solution)/shard_map/all_gather | solution.py:350
  12.7 2.2 %second.1 = (bf16[32,1152]{1,0:T(8,128)(2,1)S(1)}, bf16[64,256]{1,0:T(8,128)(2,1)S(1)}, f32[32,512]{1,0:T(8,128)S(1)}, f32[32,128]{1,0:T(8,128)S(1)}) custom-call(f32[8,128]{1,0:T(8,128)S(1)} %broadcast_in_dim.9.ridge, bf16[4,32,1536]{2,1,0:T(8,128)(2,1)S(1)} %bitcast.18, bf16[8,4,256,256]{3,2,1,0:T(8,128)(2,1)S(1)} %get-tuple-element.24.cov, ...), custom_call_target="tpu_custom_call" | custom-call | tf_op jit(solution)/shard_map/second/pallas_call | solution.py:351
  14.9 0.0 copy-start
  14.9 0.0 copy-start.1
  14.9 0.4 collective-permute-start
  15.3 0.6 %own.1.mine = f32[32,1152]{1,0:T(8,128)S(1)} custom-call(bf16[8,1024,256]{2,1,0:T(8,128)(2,1)S(1)} %get-tuple-element.22.val, bf16[64,256]{1,0:T(8,128)(2,1)S(1)} %get-tuple-element.32.lhs, f32[32,128]{1,0:T(8,128)S(1)} %get-tuple-element.28.total_in, f32[32,512]{1,0:T(8,128)S(1)} %get-tuple-element.33.low, f32[32,128]{1,0:T(8,128)S(1)} %get-tuple-element.34.share), custom_call_target="tpu_custom_call" | custom-call | flops 268435456 | bytes 2097152 | tf_op jit(solution)/shard_map/own/pallas_call | solution.py:365
  15.9 0.3 collective-permute-done.partner
  16.2 2.8 %collective-permute-start.1 = (bf16[32,1152]{1,0:T(8,128)(2,1)S(1)}, bf16[32,1152]{1,0:T(8,128)(2,1)S(1)}, u32[]{:S(2)}, u32[]{:S(2)}) collective-permute-start(bf16[32,1152]{1,0:T(8,128)(2,1)S(1)} %add_convert_fusion), channel_id=1, source_target_pairs={{0,64},{64,0},{1,65},{65,1},{2,66},{66,2},{3,67},{67,3},{4,68},{68... | collective-permute-start | bytes 221192 | tf_op jit(solution)/shard_map/ppermute | solution.py:300
  19.0 3.3 %collective-permute-done.1.arrived = bf16[32,1152]{1,0:T(8,128)(2,1)S(1)} collective-permute-done((bf16[32,1152]{1,0:T(8,128)(2,1)S(1)}, bf16[32,1152]{1,0:T(8,128)(2,1)S(1)}, u32[]{:S(2)}, u32[]{:S(2)}) %collective-permute-start.1) | collective-permute-done | bytes 73760 | tf_op jit(solution)/shard_map/ppermute | solution.py:300
  22.3 0.0 copy-done
  22.3 0.0 copy-done.1
  22.3 0.6 %third.1 = (bf16[34,32,128]{2,1,0:T(8,128)(2,1)S(1)}, bf16[32,256]{1,0:T(8,128)(2,1)S(1)}, f32[32,128]{1,0:T(8,128)S(1)}) custom-call(f32[32,1152]{1,0:T(8,128)S(1)} %own.1.mine, bf16[32,1152]{1,0:T(8,128)(2,1)S(1)} %collective-permute-done.partner, bf16[32,1152]{1,0:T(8,128)(2,1)S(1)} %collective-permute-done.1.arrived, ...), custom_call_target="tpu_custom_call" | custom-call | tf_op jit(solution)/shard_map/third/pallas_call | solution.py:376
  23.0 0.1 collective-permute-start.2
  23.0 0.5 %last.1.kept = f32[32,32,128]{2,1,0:T(8,128)S(1)} custom-call(bf16[32,256]{1,0:T(8,128)(2,1)S(1)} %get-tuple-element.36.scaled, bf16[256,8192]{1,0:T(8,128)(2,1)S(1)} %bitcast.17), custom_call_target="tpu_custom_call" | custom-call | flops 268435456 | bytes 2097152 | tf_op jit(solution)/shard_map/last/pallas_call | solution.py:388
  23.5 1.1 %collective-permute-done.2.arrived = bf16[34,32,128]{2,1,0:T(8,128)(2,1)S(1)} collective-permute-done((bf16[34,32,128]{2,1,0:T(8,128)(2,1)S(1)}, bf16[34,32,128]{2,1,0:T(8,128)(2,1)S(1)}, u32[]{:S(2)}, u32[]{:S(2)}) %collective-permute-start.2) | collective-permute-done | bytes 278560 | tf_op jit(solution)/shard_map/ppermute | solution.py:300
  24.6 0.1 join.1
  24.7 21.1 %all_to_all.5 = bf16[32,32,128]{2,1,0:T(8,128)(2,1)S(1)} all-to-all(bf16[32,32,128]{2,1,0:T(8,128)(2,1)S(1)} %join.1), channel_id=1, replica_groups=mesh['xh'=2,'core'=2,'head'=16,'batch'=2] {'xh','head'}, dimensions={0} | all-to-all | bytes 524288 | tf_op jit(solution)/shard_map/all_to_all | solution.py:405
  45.8 0.6 %reduce_sum.12 = bf16[32,128]{1,0:T(8,128)(2,1)} reduce(bf16[32,32,128]{2,1,0:T(8,128)(2,1)S(1)} %all_to_all.5, bf16[]{:T(256)} %constant.2.clone.1), dimensions={0}, to_apply=%region_0.0 | reduce | flops 126976 | bytes 270338 | tf_op jit(solution)/shard_map/reduce_sum | solution.py:406
  (2 shorter events, 0.0 us)
Async XLA Ops:
  14.9 7.5 %copy-start = (bf16[1,256,8192]{2,1,0:T(8,128)(2,1)S(1)}, bf16[1,256,8192]{2,1,0:T(8,128)(2,1)}, u32[]{:S(2)}) copy-start(bf16[1,256,8192]{2,1,0:T(8,128)(2,1)} %param.19) | copy-start | bytes 12582916
  14.9 7.5 %copy-start.1 = (f32[1,256]{1,0:T(1,128)S(1)}, f32[1,256]{1,0:T(1,128)}, u32[]{:S(2)}) copy-start(f32[1,256]{1,0:T(1,128)} %gain.1) | copy-start | bytes 3076
  14.9 1.3 %collective-permute-start = (bf16[32,1152]{1,0:T(8,128)(2,1)S(1)}, bf16[32,1152]{1,0:T(8,128)(2,1)S(1)}, u32[]{:S(2)}, u32[]{:S(2)}) collective-permute-start(bf16[32,1152]{1,0:T(8,128)(2,1)S(1)} %get-tuple-element.35), channel_id=1, source_target_pairs={{0,32},{32,0},{1,33},{33,1},{2,34},{34,2},{3,35},{35,3},{4,36},{36... | collective-permute-start | bytes 221192 | tf_op jit(solution)/shard_map/ppermute | solution.py:300
  16.2 6.1 %collective-permute-start.1 = (bf16[32,1152]{1,0:T(8,128)(2,1)S(1)}, bf16[32,1152]{1,0:T(8,128)(2,1)S(1)}, u32[]{:S(2)}, u32[]{:S(2)}) collective-permute-start(bf16[32,1152]{1,0:T(8,128)(2,1)S(1)} %add_convert_fusion), channel_id=1, source_target_pairs={{0,64},{64,0},{1,65},{65,1},{2,66},{66,2},{3,67},{67,3},{4,68},{68... | collective-permute-start | bytes 221192 | tf_op jit(solution)/shard_map/ppermute | solution.py:300
  23.0 1.6 %collective-permute-start.2 = (bf16[34,32,128]{2,1,0:T(8,128)(2,1)S(1)}, bf16[34,32,128]{2,1,0:T(8,128)(2,1)S(1)}, u32[]{:S(2)}, u32[]{:S(2)}) collective-permute-start(bf16[34,32,128]{2,1,0:T(8,128)(2,1)S(1)} %get-tuple-element.37), channel_id=1, source_target_pairs={{0,32},{32,0},{1,33},{33,1},{2,34},{34,2},{3,35},{35,3},{4,36},{36... | collective-permute-start | bytes 835592 | tf_op jit(solution)/shard_map/ppermute | solution.py:300

commit v6 on v5

--- a/solution.py
+++ b/solution.py
@@ -85,7 +85,7 @@
 ):
     me, core, xh = position()
     start = pl.multiple_of(me * PART, PART)
-    across = pl.multiple_of((2 * (1 - xh) + core) * PART, PART)
+    across = pl.multiple_of((2 * (1 - xh) + 1 - core) * PART, PART)
     ends = [
         (decay_hbm, decay_in),
         (write_hbm, write_in),
@@ -239,8 +239,8 @@
     rows = slice(8 * p, 8 * p + 8)
     first = lax.broadcasted_iota(jnp.int32, (8, 1), 0) < DRAFT
     both = lhs[16 * p : 16 * p + 16, :]
-    for slot, x in enumerate((xh, 1 - xh)):
-        entries = pl.ds(pl.multiple_of((2 * x + core) * PART, PART), PART)
+    for slot, part in enumerate((2 * xh + core, 2 * (1 - xh) + 1 - core)):
+        entries = pl.ds(pl.multiple_of(part * PART, PART), PART)
         res = [mm(both, val[2 * p + n, entries, :], NT) for n in range(2)]
         for m in range(2):
             half = slice(8 * m, 8 * m + 8)
@@ -372,7 +372,8 @@
         cost_estimate=estimate,
     )(carried[1], lhs, carried[5], low, share)
     partner = swapped(sent, "core")
-    other = swapped((kept + partner.astype(F32)).astype(BF16), "xh")
+    pair = (kept + partner.astype(F32)).astype(BF16)
+    other = lax.ppermute(pair, KEY, [(n, n ^ 3) for n in range(4)])
     sent, scaled, squares = pl.pallas_call(
         third_kernel,
         name="third",

time: 46.6 us -> 46.3 us (level)
  waiting for transfers between devices: 4.69 us -> 3.92 us
    ppermute x3 -> x2, waiting for transfers between devices: 4.69 us -> 1.01 us  [swapped(): return lax.ppermute(x, axis, [(0, 1), (1, 0)])]
    ppermute x0 -> x1, waiting for transfers between devices: none -> 2.9 us  [body(): other = lax.ppermute(pair, KEY, [(n, n ^ 3) for n in range(4)])]
    ppermute x0 -> x1, starting transfers between devices: none -> 2.72 us  [body(): other = lax.ppermute(pair, KEY, [(n, n ^ 3) for n in range(4)])]
    ppermute x3 -> x2, starting transfers between devices: 3.24 us -> 0.83 us  [swapped(): return lax.ppermute(x, axis, [(0, 1), (1, 0)])]
where the time goes in v6:
time: 46.3 us; the launch traced here: 46.1 us
  blocking collectives  29.4 us (63%)
  Pallas kernels  7.9 us (17%)
  waiting for transfers between devices  3.92 us (8%)
  starting transfers between devices  3.55 us (8%)
  between operations  0.68 us (1%)
  other arithmetic  0.66 us (1%)
    all_to_all x1, blocking collectives, body(): landed = lax.all_to_all(part, ('xh', 'head'), 0, 0, tiled=True)  21.3 us
    all_gather x1, blocking collectives, body(): gathered = lax.all_gather(msg, KEY)  8.1 us
    pallas_call x1, Pallas kernels, body(): pl.pallas_call(first_kernel, name='first', out_shape=(pltpu.VMEM((ROWS, D...  3.89 us
    ppermute x1, waiting for transfers between devices, body(): other = lax.ppermute(pair, KEY, [(n, n ^ 3) for n in range(4)])  2.9 us
    ppermute x1, starting transfers between devices, body(): other = lax.ppermute(pair, KEY, [(n, n ^ 3) for n in range(4)])  2.72 us
    pallas_call x1, Pallas kernels, body(): pl.pallas_call(second_kernel, name='second', out_shape=(pltpu.VMEM((ROWS,...  2.21 us
    ppermute x2, waiting for transfers between devices, swapped(): return lax.ppermute(x, axis, [(0, 1), (1, 0)])  1.01 us
  transfers between devices with their start and end apart: 3, of which 3 were waited for; matrix products, arithmetic and copies ran while one was open for 0% of the time, Pallas kernels for 2%

profile of v6, /device:TPU:0, one launch (start us, length us, event | category | flops | bytes accessed | tf_op | source)
XLA Modules:
  0.0 46.1 jit_solution(13569902270154966654)
XLA Ops:
  0.7 3.9 %first.1 = (bf16[32,1536]{1,0:T(8,128)(2,1)S(1)}, bf16[8,4,256,256]{3,2,1,0:T(8,128)(2,1)S(1)}, bf16[8,1024,256]{2,1,0:T(8,128)(2,1)S(1)}, f32[32,1024]{1,0:T(8,...) custom-call(bf16[8,4,1024]{2,1,0:T(4,128)(2,1)} %bitcast.21, ...), custom_call_target="tpu_custom_call" | custom-call | tf_op jit(solution)/shard_map/first/pallas_call | solution.py:320
  4.5 8.1 %all-gather = bf16[128,1536]{1,0:T(8,128)(2,1)S(1)} all-gather(bf16[32,1536]{1,0:T(8,128)(2,1)S(1)} %get-tuple-element.23), channel_id=2, replica_groups=mesh['xh'=2,'core'=2,'head'=16,'batch'=2] {'xh','core'}, dimensions={0}, use_global_device_ids=true | all-gather | bytes 491520 | tf_op jit(solution)/shard_map/all_gather | solution.py:350
  12.7 2.2 %second.1 = (bf16[32,1152]{1,0:T(8,128)(2,1)S(1)}, bf16[64,256]{1,0:T(8,128)(2,1)S(1)}, f32[32,512]{1,0:T(8,128)S(1)}, f32[32,128]{1,0:T(8,128)S(1)}) custom-call(f32[8,128]{1,0:T(8,128)S(1)} %broadcast_in_dim.9.ridge, bf16[4,32,1536]{2,1,0:T(8,128)(2,1)S(1)} %bitcast.18, bf16[8,4,256,256]{3,2,1,0:T(8,128)(2,1)S(1)} %get-tuple-element.24.cov, ...), custom_call_target="tpu_custom_call" | custom-call | tf_op jit(solution)/shard_map/second/pallas_call | solution.py:351
  14.9 0.0 copy-start
  14.9 0.0 copy-start.1
  14.9 0.4 collective-permute-start
  15.3 0.6 %own.1.mine = f32[32,1152]{1,0:T(8,128)S(1)} custom-call(bf16[8,1024,256]{2,1,0:T(8,128)(2,1)S(1)} %get-tuple-element.22.val, bf16[64,256]{1,0:T(8,128)(2,1)S(1)} %get-tuple-element.32.lhs, f32[32,128]{1,0:T(8,128)S(1)} %get-tuple-element.28.total_in, f32[32,512]{1,0:T(8,128)S(1)} %get-tuple-element.33.low, f32[32,128]{1,0:T(8,128)S(1)} %get-tuple-element.34.share), custom_call_target="tpu_custom_call" | custom-call | flops 268435456 | bytes 2097152 | tf_op jit(solution)/shard_map/own/pallas_call | solution.py:365
  15.9 0.3 collective-permute-done.partner
  16.2 2.7 %collective-permute-start.1 = (bf16[32,1152]{1,0:T(8,128)(2,1)S(1)}, bf16[32,1152]{1,0:T(8,128)(2,1)S(1)}, u32[]{:S(2)}, u32[]{:S(2)}) collective-permute-start(bf16[32,1152]{1,0:T(8,128)(2,1)S(1)} %add_convert_fusion), channel_id=1, source_target_pairs={{0,96},{32,64},{64,32},{96,0},{1,97},{33,65},{65,33},{97,1},{2,98}... | collective-permute-start | bytes 221192 | tf_op jit(solution)/shard_map/ppermute | solution.py:376
  18.9 2.9 %collective-permute-done.1.arrived = bf16[32,1152]{1,0:T(8,128)(2,1)S(1)} collective-permute-done((bf16[32,1152]{1,0:T(8,128)(2,1)S(1)}, bf16[32,1152]{1,0:T(8,128)(2,1)S(1)}, u32[]{:S(2)}, u32[]{:S(2)}) %collective-permute-start.1) | collective-permute-done | bytes 73760 | tf_op jit(solution)/shard_map/ppermute | solution.py:376
  21.8 0.0 copy-done
  21.8 0.0 copy-done.1
  21.8 0.6 %third.1 = (bf16[34,32,128]{2,1,0:T(8,128)(2,1)S(1)}, bf16[32,256]{1,0:T(8,128)(2,1)S(1)}, f32[32,128]{1,0:T(8,128)S(1)}) custom-call(f32[32,1152]{1,0:T(8,128)S(1)} %own.1.mine, bf16[32,1152]{1,0:T(8,128)(2,1)S(1)} %collective-permute-done.partner, bf16[32,1152]{1,0:T(8,128)(2,1)S(1)} %collective-permute-done.1.arrived, ...), custom_call_target="tpu_custom_call" | custom-call | tf_op jit(solution)/shard_map/third/pallas_call | solution.py:377
  22.5 0.4 collective-permute-start.2
  22.9 0.5 %last.1.kept = f32[32,32,128]{2,1,0:T(8,128)S(1)} custom-call(bf16[32,256]{1,0:T(8,128)(2,1)S(1)} %get-tuple-element.36.scaled, bf16[256,8192]{1,0:T(8,128)(2,1)S(1)} %bitcast.17), custom_call_target="tpu_custom_call" | custom-call | flops 268435456 | bytes 2097152 | tf_op jit(solution)/shard_map/last/pallas_call | solution.py:389
  23.4 0.7 %collective-permute-done.2.arrived = bf16[34,32,128]{2,1,0:T(8,128)(2,1)S(1)} collective-permute-done((bf16[34,32,128]{2,1,0:T(8,128)(2,1)S(1)}, bf16[34,32,128]{2,1,0:T(8,128)(2,1)S(1)}, u32[]{:S(2)}, u32[]{:S(2)}) %collective-permute-start.2) | collective-permute-done | bytes 278560 | tf_op jit(solution)/shard_map/ppermute | solution.py:300
  24.1 0.1 join.1
  24.2 21.3 %all_to_all.5 = bf16[32,32,128]{2,1,0:T(8,128)(2,1)S(1)} all-to-all(bf16[32,32,128]{2,1,0:T(8,128)(2,1)S(1)} %join.1), channel_id=1, replica_groups=mesh['xh'=2,'core'=2,'head'=16,'batch'=2] {'xh','head'}, dimensions={0} | all-to-all | bytes 524288 | tf_op jit(solution)/shard_map/all_to_all | solution.py:406
  45.5 0.6 %reduce_sum.12 = bf16[32,128]{1,0:T(8,128)(2,1)} reduce(bf16[32,32,128]{2,1,0:T(8,128)(2,1)S(1)} %all_to_all.5, bf16[]{:T(256)} %constant.2.clone.1), dimensions={0}, to_apply=%region_0.0 | reduce | flops 126976 | bytes 270338 | tf_op jit(solution)/shard_map/reduce_sum | solution.py:407
  (2 shorter events, 0.0 us)
Async XLA Ops:
  14.9 7.0 %copy-start = (bf16[1,256,8192]{2,1,0:T(8,128)(2,1)S(1)}, bf16[1,256,8192]{2,1,0:T(8,128)(2,1)}, u32[]{:S(2)}) copy-start(bf16[1,256,8192]{2,1,0:T(8,128)(2,1)} %param.19) | copy-start | bytes 12582916
  14.9 7.0 %copy-start.1 = (f32[1,256]{1,0:T(1,128)S(1)}, f32[1,256]{1,0:T(1,128)}, u32[]{:S(2)}) copy-start(f32[1,256]{1,0:T(1,128)} %gain.1) | copy-start | bytes 3076
  14.9 1.3 %collective-permute-start = (bf16[32,1152]{1,0:T(8,128)(2,1)S(1)}, bf16[32,1152]{1,0:T(8,128)(2,1)S(1)}, u32[]{:S(2)}, u32[]{:S(2)}) collective-permute-start(bf16[32,1152]{1,0:T(8,128)(2,1)S(1)} %get-tuple-element.35), channel_id=1, source_target_pairs={{0,32},{32,0},{1,33},{33,1},{2,34},{34,2},{3,35},{35,3},{4,36},{36... | collective-permute-start | bytes 221192 | tf_op jit(solution)/shard_map/ppermute | solution.py:300
  16.2 5.6 %collective-permute-start.1 = (bf16[32,1152]{1,0:T(8,128)(2,1)S(1)}, bf16[32,1152]{1,0:T(8,128)(2,1)S(1)}, u32[]{:S(2)}, u32[]{:S(2)}) collective-permute-start(bf16[32,1152]{1,0:T(8,128)(2,1)S(1)} %add_convert_fusion), channel_id=1, source_target_pairs={{0,96},{32,64},{64,32},{96,0},{1,97},{33,65},{65,33},{97,1},{2,98}... | collective-permute-start | bytes 221192 | tf_op jit(solution)/shard_map/ppermute | solution.py:376
  22.5 1.6 %collective-permute-start.2 = (bf16[34,32,128]{2,1,0:T(8,128)(2,1)S(1)}, bf16[34,32,128]{2,1,0:T(8,128)(2,1)S(1)}, u32[]{:S(2)}, u32[]{:S(2)}) collective-permute-start(bf16[34,32,128]{2,1,0:T(8,128)(2,1)S(1)} %get-tuple-element.37), channel_id=1, source_target_pairs={{0,32},{32,0},{1,33},{33,1},{2,34},{34,2},{3,35},{35,3},{4,36},{36... | collective-permute-start | bytes 835592 | tf_op jit(solution)/shard_map/ppermute | solution.py:300

commit v7 on v6

--- a/solution.py
+++ b/solution.py
@@ -152,8 +152,8 @@
 
 
 def second_kernel(
-    ridge, gathered, cov, val, q32, k32, values_in, total_in, mix_in, ck, cq, sent, lhs, low, share_out,
-    p32, c32, y32, w32, low32, d32, x32, ap32, ac32, dm32,
+    ridge, gathered, cov, val, q32, k32, values_in, total_in, mix_in, ck, cq, sent, lhs, share_out, d32, x32,
+    p32, c32, y32, w32, low32, ap32, ac32, dm32,
 ):
     total, shift, mix = total_in[:, :1], ridge[0:1, 0:1], mix_in[...]
     me, core, xh = position()
@@ -226,13 +226,8 @@
         rows = slice(8 * p, 8 * p + 8)
         both = [x32[rows, mine].astype(BF16), dm32[rows, :].astype(BF16)]
         lhs[2 * 8 * p : 2 * 8 * (p + 1), :] = jnp.concatenate(both, axis=0)
-        if p == 2:
-            dots = mm(jnp.concatenate(halves(x32[...]) + (d32[...].astype(BF16),), axis=0), keys, NT)
         by_values(lhs, val, total, xh, 1 - core, p, sent)
     sent[:, SHARE:] = share.astype(BF16)
-    values = values_in[:, :PART].astype(BF16)
-    low[:, :PART] = mm_wide(mix * (dots[:ROWS] + dots[ROWS : 2 * ROWS]), values)
-    low[:, PART:] = mm_wide(mix * dots[2 * ROWS :], values)
 
 
 def by_values(lhs, val, total, xh, core, p, out):
@@ -249,13 +244,19 @@
             out[rows, at : at + PART] = part.astype(out.dtype)
 
 
-def own_kernel(val, lhs, total_in, low, share, kept):
+def own_kernel(val, lhs, total_in, mix_in, values_in, k32, share, d32, x32, kept):
     _, core, xh = position()
-    total = total_in[:, :1]
+    total, mix = total_in[:, :1], mix_in[...]
+    keys, values = k32[...].astype(BF16), values_in[:, :PART].astype(BF16)
+    dots = mm(jnp.concatenate(halves(x32[...]) + (d32[...].astype(BF16),), axis=0), keys, NT)
     for p in range(SEQS // 2):
         by_values(lhs, val, total, xh, core, p, kept)
+        if p == 1:
+            low = [mm_wide(mix * (dots[:ROWS] + dots[ROWS : 2 * ROWS]), values)]
+            low.append(mm_wide(mix * dots[2 * ROWS :], values))
     kept[:, SHARE:] = share[...]
-    kept[:, : 2 * PART] += low[...]
+    for m in range(2):
+        kept[:, m * PART : (m + 1) * PART] += low[m]
 
 
 def project(scaled, weight, core, out):
@@ -348,29 +349,31 @@
         compiler_params=params(16),
     )(*in_hbm)
     gathered = lax.all_gather(msg, KEY)
-    sent, lhs, low, share = pl.pallas_call(
+    total, mix = carried[5:7]
+    sent, lhs, share, direction, found = pl.pallas_call(
         second_kernel,
         name="second",
         out_shape=(
             pltpu.VMEM((ROWS, SHARE + 128), BF16),
             pltpu.VMEM((2 * ROWS, PART), BF16),
-            pltpu.VMEM((ROWS, 2 * PART), F32),
             pltpu.VMEM((ROWS, 128), F32),
+            pltpu.VMEM((ROWS, DK), F32),
+            pltpu.VMEM((ROWS, DK), F32),
         ),
         in_specs=[VMEM] * 11,
-        out_specs=(VMEM,) * 4,
-        scratch_shapes=[pltpu.VMEM((ROWS, n), F32) for n in [DK] * 7 + [PART] * 3],
+        out_specs=(VMEM,) * 5,
+        scratch_shapes=[pltpu.VMEM((ROWS, n), F32) for n in [DK] * 5 + [PART] * 3],
         compiler_params=params(16),
     )(jnp.broadcast_to(ridge_shift[None], (8, 128)), gathered, *carried)
     kept = pl.pallas_call(
         own_kernel,
         name="own",
         out_shape=pltpu.VMEM((ROWS, SHARE + 128), F32),
-        in_specs=[VMEM] * 5,
+        in_specs=[VMEM] * 9,
         out_specs=VMEM,
         compiler_params=params(16),
         cost_estimate=estimate,
-    )(carried[1], lhs, carried[5], low, share)
+    )(carried[1], lhs, total, mix, carried[4], carried[3], share, direction, found)
     partner = swapped(sent, "core")
     pair = (kept + partner.astype(F32)).astype(BF16)
     other = lax.ppermute(pair, KEY, [(n, n ^ 3) for n in range(4)])

time: 46.3 us -> 46.2 us (level)
  no operation moved by 1% of the time
where the time goes in v7:
time: 46.2 us; the launch traced here: 46 us
  blocking collectives  29.4 us (64%)
  Pallas kernels  7.84 us (17%)
  waiting for transfers between devices  3.88 us (8%)
  starting transfers between devices  3.55 us (8%)
  between operations  0.68 us (1%)
  other arithmetic  0.66 us (1%)
    all_to_all x1, blocking collectives, body(): landed = lax.all_to_all(part, ('xh', 'head'), 0, 0, tiled=True)  21.3 us
    all_gather x1, blocking collectives, body(): gathered = lax.all_gather(msg, KEY)  8.1 us
    pallas_call x1, Pallas kernels, body(): pl.pallas_call(first_kernel, name='first', out_shape=(pltpu.VMEM((ROWS, D...  3.89 us
    ppermute x1, waiting for transfers between devices, body(): other = lax.ppermute(pair, KEY, [(n, n ^ 3) for n in range(4)])  2.91 us
    ppermute x1, starting transfers between devices, body(): other = lax.ppermute(pair, KEY, [(n, n ^ 3) for n in range(4)])  2.71 us
    pallas_call x1, Pallas kernels, body(): pl.pallas_call(second_kernel, name='second', out_shape=(pltpu.VMEM((ROWS,...  2.11 us
    ppermute x2, waiting for transfers between devices, swapped(): return lax.ppermute(x, axis, [(0, 1), (1, 0)])  0.97 us
  transfers between devices with their start and end apart: 3, of which 3 were waited for; matrix products, arithmetic and copies ran while one was open for 0% of the time, Pallas kernels for 2%

profile of v7, /device:TPU:0, one launch (start us, length us, event | category | flops | bytes accessed | tf_op | source)
XLA Modules:
  0.0 46.0 jit_solution(3446179786890303632)
XLA Ops:
  0.7 3.9 %first.1 = (bf16[32,1536]{1,0:T(8,128)(2,1)S(1)}, bf16[8,4,256,256]{3,2,1,0:T(8,128)(2,1)S(1)}, bf16[8,1024,256]{2,1,0:T(8,128)(2,1)S(1)}, f32[32,1024]{1,0:T(8,...) custom-call(bf16[8,4,1024]{2,1,0:T(4,128)(2,1)} %bitcast.21, ...), custom_call_target="tpu_custom_call" | custom-call | tf_op jit(solution)/shard_map/first/pallas_call | solution.py:321
  4.5 8.1 %all-gather = bf16[128,1536]{1,0:T(8,128)(2,1)S(1)} all-gather(bf16[32,1536]{1,0:T(8,128)(2,1)S(1)} %get-tuple-element.24), channel_id=2, replica_groups=mesh['xh'=2,'core'=2,'head'=16,'batch'=2] {'xh','core'}, dimensions={0}, use_global_device_ids=true | all-gather | bytes 491520 | tf_op jit(solution)/shard_map/all_gather | solution.py:351
  12.7 2.1 %second.1 = (bf16[32,1152]{1,0:T(8,128)(2,1)S(1)}, bf16[64,256]{1,0:T(8,128)(2,1)S(1)}, f32[32,128]{1,0:T(8,128)S(1)}, f32[32,1024]{1,0:T(8,128)S(1)}, f32[32,1024]{1,0:T(8,128)S(1)}) custom-call(f32[8,128]{1,0:T(8,128)S(1)} %broadcast_in_dim.9.ridge, bf16[4,32,1536]{2,1,0:T(8,128)(2,1)S(1)} %bitcast.18, bf16[8,4,256,256]{3,2,1,0:T(8,128)(2,1)S(1)} %get-tuple-element.25.cov, ...), custom_call_target="tpu_custom_call" | custom-call | tf_op jit(solution)/shard_map/second/pallas_call | solution.py:353
  14.8 0.0 copy-start
  14.8 0.0 copy-start.1
  14.8 0.4 collective-permute-start
  15.2 0.7 %own.1.mine = f32[32,1152]{1,0:T(8,128)S(1)} custom-call(bf16[8,1024,256]{2,1,0:T(8,128)(2,1)S(1)} %get-tuple-element.23.val, bf16[64,256]{1,0:T(8,128)(2,1)S(1)} %get-tuple-element.33.lhs, f32[32,128]{1,0:T(8,128)S(1)} %get-tuple-element.29.total_in, f32[32,32]{1,0:T(8,128)S(1)} %get-tuple-element.30.mix_in, ...), custom_call_target="tpu_custom_call" | custom-call | flops 268435456 | bytes 2097152 | tf_op jit(solution)/shard_map/own/pallas_call | solution.py:368
  15.9 0.2 collective-permute-done.partner
  16.1 2.7 %collective-permute-start.1 = (bf16[32,1152]{1,0:T(8,128)(2,1)S(1)}, bf16[32,1152]{1,0:T(8,128)(2,1)S(1)}, u32[]{:S(2)}, u32[]{:S(2)}) collective-permute-start(bf16[32,1152]{1,0:T(8,128)(2,1)S(1)} %add_convert_fusion), channel_id=1, source_target_pairs={{0,96},{32,64},{64,32},{96,0},{1,97},{33,65},{65,33},{97,1},{2,98}... | collective-permute-start | bytes 221192 | tf_op jit(solution)/shard_map/ppermute | solution.py:379
  18.8 2.9 %collective-permute-done.1.arrived = bf16[32,1152]{1,0:T(8,128)(2,1)S(1)} collective-permute-done((bf16[32,1152]{1,0:T(8,128)(2,1)S(1)}, bf16[32,1152]{1,0:T(8,128)(2,1)S(1)}, u32[]{:S(2)}, u32[]{:S(2)}) %collective-permute-start.1) | collective-permute-done | bytes 73760 | tf_op jit(solution)/shard_map/ppermute | solution.py:379
  21.7 0.0 copy-done
  21.7 0.0 copy-done.1
  21.7 0.6 %third.1 = (bf16[34,32,128]{2,1,0:T(8,128)(2,1)S(1)}, bf16[32,256]{1,0:T(8,128)(2,1)S(1)}, f32[32,128]{1,0:T(8,128)S(1)}) custom-call(f32[32,1152]{1,0:T(8,128)S(1)} %own.1.mine, bf16[32,1152]{1,0:T(8,128)(2,1)S(1)} %collective-permute-done.partner, bf16[32,1152]{1,0:T(8,128)(2,1)S(1)} %collective-permute-done.1.arrived, ...), custom_call_target="tpu_custom_call" | custom-call | tf_op jit(solution)/shard_map/third/pallas_call | solution.py:380
  22.4 0.4 collective-permute-start.2
  22.8 0.5 %last.1.kept = f32[32,32,128]{2,1,0:T(8,128)S(1)} custom-call(bf16[32,256]{1,0:T(8,128)(2,1)S(1)} %get-tuple-element.38.scaled, bf16[256,8192]{1,0:T(8,128)(2,1)S(1)} %bitcast.17), custom_call_target="tpu_custom_call" | custom-call | flops 268435456 | bytes 2097152 | tf_op jit(solution)/shard_map/last/pallas_call | solution.py:392
  23.3 0.7 %collective-permute-done.2.arrived = bf16[34,32,128]{2,1,0:T(8,128)(2,1)S(1)} collective-permute-done((bf16[34,32,128]{2,1,0:T(8,128)(2,1)S(1)}, bf16[34,32,128]{2,1,0:T(8,128)(2,1)S(1)}, u32[]{:S(2)}, u32[]{:S(2)}) %collective-permute-start.2) | collective-permute-done | bytes 278560 | tf_op jit(solution)/shard_map/ppermute | solution.py:301
  24.0 0.1 join.1
  24.1 21.3 %all_to_all.5 = bf16[32,32,128]{2,1,0:T(8,128)(2,1)S(1)} all-to-all(bf16[32,32,128]{2,1,0:T(8,128)(2,1)S(1)} %join.1), channel_id=1, replica_groups=mesh['xh'=2,'core'=2,'head'=16,'batch'=2] {'xh','head'}, dimensions={0} | all-to-all | bytes 524288 | tf_op jit(solution)/shard_map/all_to_all | solution.py:409
  45.4 0.6 %reduce_sum.12 = bf16[32,128]{1,0:T(8,128)(2,1)} reduce(bf16[32,32,128]{2,1,0:T(8,128)(2,1)S(1)} %all_to_all.5, bf16[]{:T(256)} %constant.2.clone.1), dimensions={0}, to_apply=%region_0.0 | reduce | flops 126976 | bytes 270338 | tf_op jit(solution)/shard_map/reduce_sum | solution.py:410
  (2 shorter events, 0.0 us)
Async XLA Ops:
  14.8 7.0 %copy-start = (bf16[1,256,8192]{2,1,0:T(8,128)(2,1)S(1)}, bf16[1,256,8192]{2,1,0:T(8,128)(2,1)}, u32[]{:S(2)}) copy-start(bf16[1,256,8192]{2,1,0:T(8,128)(2,1)} %param.19) | copy-start | bytes 12582916
  14.8 7.0 %copy-start.1 = (f32[1,256]{1,0:T(1,128)S(1)}, f32[1,256]{1,0:T(1,128)}, u32[]{:S(2)}) copy-start(f32[1,256]{1,0:T(1,128)} %gain.1) | copy-start | bytes 3076
  14.8 1.3 %collective-permute-start = (bf16[32,1152]{1,0:T(8,128)(2,1)S(1)}, bf16[32,1152]{1,0:T(8,128)(2,1)S(1)}, u32[]{:S(2)}, u32[]{:S(2)}) collective-permute-start(bf16[32,1152]{1,0:T(8,128)(2,1)S(1)} %get-tuple-element.37), channel_id=1, source_target_pairs={{0,32},{32,0},{1,33},{33,1},{2,34},{34,2},{3,35},{35,3},{4,36},{36... | collective-permute-start | bytes 221192 | tf_op jit(solution)/shard_map/ppermute | solution.py:301
  16.1 5.6 %collective-permute-start.1 = (bf16[32,1152]{1,0:T(8,128)(2,1)S(1)}, bf16[32,1152]{1,0:T(8,128)(2,1)S(1)}, u32[]{:S(2)}, u32[]{:S(2)}) collective-permute-start(bf16[32,1152]{1,0:T(8,128)(2,1)S(1)} %add_convert_fusion), channel_id=1, source_target_pairs={{0,96},{32,64},{64,32},{96,0},{1,97},{33,65},{65,33},{97,1},{2,98}... | collective-permute-start | bytes 221192 | tf_op jit(solution)/shard_map/ppermute | solution.py:379
  22.4 1.6 %collective-permute-start.2 = (bf16[34,32,128]{2,1,0:T(8,128)(2,1)S(1)}, bf16[34,32,128]{2,1,0:T(8,128)(2,1)S(1)}, u32[]{:S(2)}, u32[]{:S(2)}) collective-permute-start(bf16[34,32,128]{2,1,0:T(8,128)(2,1)S(1)} %get-tuple-element.39), channel_id=1, source_target_pairs={{0,32},{32,0},{1,33},{33,1},{2,34},{34,2},{3,35},{35,3},{4,36},{36... | collective-permute-start | bytes 835592 | tf_op jit(solution)/shard_map/ppermute | solution.py:301
